TPU v7x, 8 devices: a whole 2x2x1 slice. The times are simulated.
8 devices in a mesh: fsdp: 4 (over z, y, x), ep: 2 (over core).
Axes of the slice: x: 2, y: 2, z: 1, core: 2. Of those that a mesh axis runs over, the one named last changes fastest.
Arguments:
- x_in: bfloat16 [2, 16384, 768], P(None, ('fsdp', 'ep'))
- dy_out: bfloat16 [2, 16384, 768], P(None, ('fsdp', 'ep'))
- expert_idx: int32 [2, 16384, 2], P(None, ('fsdp', 'ep'))
- gate_prob: float32 [2, 16384, 2], P(None, ('fsdp', 'ep'))
- w_one: bfloat16 [8, 768, 4096], P('ep', 'fsdp')
- w_two: bfloat16 [8, 4096, 768], P('ep', None, 'fsdp')
- w_three: bfloat16 [8, 768, 4096], P('ep', 'fsdp')
Outputs:
- output 1: bfloat16 [2, 16384, 768], P(None, ('fsdp', 'ep'))
- output 2: float32 [2, 16384, 2], P(None, ('fsdp', 'ep'))
- output 3: float32 [8, 768, 4096], P('ep', 'fsdp')
- output 4: float32 [8, 4096, 768], P('ep', None, 'fsdp')
- output 5: float32 [8, 768, 4096], P('ep', 'fsdp')
All inputs are finite; a program needn't handle non-finite values.
Results may differ from a plain program's by a relative error of at most 0.001.
Values are sent between devices in bfloat16 or wider.
A program may use at most 1 GiB of HBM per device.

v0:
```python
import functools

import jax
import jax.numpy as jnp
from jax import lax
from jax.experimental import pallas as pl
from jax.experimental.pallas import tpu as pltpu
from jax.sharding import PartitionSpec as P


BLOCKS = 4
HALVES = 2
TILE = 512
CHUNK = 256
ALIGN = 16
LANES = 128
BF16 = jnp.bfloat16
F32 = jnp.float32
I32 = jnp.int32
BOTH = ('fsdp', 'ep')
ANY = pl.BlockSpec(memory_space=pl.ANY)


def capacity_of(tok_rows, top_k, experts):
    return 8 * ((5 * tok_rows * top_k + 32 * experts - 1) // (32 * experts))


def swap(value, axes, shift, devices):
    if shift == 0:
        return value
    return lax.ppermute(value, axes, [(s, s ^ shift) for s in range(devices)])


def matmul(left, right):
    return jnp.dot(left, right, preferred_element_type=F32)


def matmul_nt(left, right):
    return lax.dot_general(left, right, (((1,), (1,)), ((), ())), preferred_element_type=F32)


def params():
    return pltpu.CompilerParams(vmem_limit_bytes=60 * 2**20, dimension_semantics=None)


def pack_kernel(pieces, d_model, place, *refs):
    tok_refs, gates_ref, out_ref = refs[:pieces], refs[pieces], refs[pieces + 1]
    tok, gates, gated, in_sem, gate_sem, out_sem = refs[pieces + 2:]
    gate_copy = pltpu.make_async_copy(gates_ref, gates, gate_sem)
    gate_copy.start()
    loads = [pltpu.make_async_copy(tok_refs[k], tok.at[k], in_sem.at[k]) for k in range(pieces)]
    for load in loads:
        load.start()
    gate_copy.wait()

    def stores(k):
        first = pl.multiple_of(place[0, k], ALIGN)
        size = pl.multiple_of(place[1, k], ALIGN)
        used, rows = pl.ds(0, size), pl.ds(first, size)
        return [
            pltpu.make_async_copy(tok.at[k, used, :], out_ref.at[rows, pl.ds(0, 2 * d_model)], out_sem.at[k, 0]),
            pltpu.make_async_copy(gated.at[k, used, :], out_ref.at[rows, pl.ds(2 * d_model, d_model)], out_sem.at[k, 1]),
        ]

    for k in range(pieces):
        loads[k].wait()

        @pl.when(place[1, k] > 0)
        def _():
            for c in range(d_model // LANES):
                dy = tok[k, :, pl.ds(d_model + c * LANES, LANES)].astype(F32)
                gated[k, :, pl.ds(c * LANES, LANES)] = (gates[k] * dy).astype(BF16)
            for store in stores(k):
                store.start()

    for k in range(pieces):
        @pl.when(place[1, k] > 0)
        def _():
            for store in stores(k):
                store.wait()


def pack(place, tokens, gates, capacity, d_model):
    pieces = len(tokens)
    return pl.pallas_call(
        functools.partial(pack_kernel, pieces, d_model),
        out_shape=jax.ShapeDtypeStruct((pieces * capacity, 3 * d_model), BF16),
        in_specs=[pl.BlockSpec(memory_space=pltpu.SMEM)] + [ANY] * (pieces + 1),
        out_specs=ANY,
        scratch_shapes=[
            pltpu.VMEM((pieces, capacity, 2 * d_model), BF16),
            pltpu.VMEM((pieces, capacity, LANES), F32),
            pltpu.VMEM((pieces, capacity, d_model), BF16),
            pltpu.SemaphoreType.DMA((pieces,)),
            pltpu.SemaphoreType.DMA,
            pltpu.SemaphoreType.DMA((pieces, 2)),
        ],
        compiler_params=params(),
        cost_estimate=pl.CostEstimate(flops=10**9, bytes_accessed=40 * 2**20, transcendentals=0),
        name='pack',
    )(place, *tokens, gates)


def unpack_kernel(pieces, place, packed_ref, *refs):
    out_refs = refs[:pieces]
    rows_ref, in_sem, out_sem = refs[pieces:]
    load = pltpu.make_async_copy(packed_ref, rows_ref, in_sem)
    load.start()
    load.wait()

    def store(k):
        first = pl.multiple_of(place[0, k], ALIGN)
        size = pl.multiple_of(place[1, k], ALIGN)
        return pltpu.make_async_copy(rows_ref.at[pl.ds(first, size), :], out_refs[k].at[pl.ds(0, size), :], out_sem.at[k])

    for k in range(pieces):
        @pl.when(place[1, k] > 0)
        def _():
            store(k).start()
    for k in range(pieces):
        @pl.when(place[1, k] > 0)
        def _():
            store(k).wait()


def unpack(place, packed, pieces, capacity):
    d_model = packed.shape[1]
    return pl.pallas_call(
        functools.partial(unpack_kernel, pieces),
        out_shape=[jax.ShapeDtypeStruct((capacity, d_model), packed.dtype)] * pieces,
        in_specs=[pl.BlockSpec(memory_space=pltpu.SMEM), ANY],
        out_specs=[ANY] * pieces,
        scratch_shapes=[pltpu.VMEM(packed.shape, packed.dtype), pltpu.SemaphoreType.DMA, pltpu.SemaphoreType.DMA((pieces,))],
        compiler_params=params(),
        cost_estimate=pl.CostEstimate(flops=10**9, bytes_accessed=16 * 2**20, transcendentals=0),
        name='unpack',
    )(place, packed)


def expert_kernel(shards, d_model, width, first_col, first, carry, info, *refs):
    refs = list(refs)
    tok_ref = refs.pop(0)
    w_refs = [refs.pop(0) for _ in range(shards)]
    dx_in, dg_in = (None, None) if first else (refs.pop(0), refs.pop(0))
    old_refs = [refs.pop(0) for _ in range(shards)] if carry else []
    dx_out, dg_out = refs.pop(0), refs.pop(0)
    grad_refs = [refs.pop(0) for _ in range(shards)]
    w_mem, grads, x_t, g_t, dx_sum, w_sem, grad_sem = refs
    d_shard = d_model // shards
    step = pl.program_id(0)
    tiles, total, my_shard = info[0], info[1], info[2]

    def shard_rows(k):
        return pl.ds(pl.multiple_of((my_shard ^ k) * d_shard, ALIGN), d_shard)

    w_copies = [pltpu.make_async_copy(w_refs[k].at[:, :, pl.ds(first_col, width)], w_mem.at[:, shard_rows(k), :], w_sem.at[k]) for k in range(shards)]
    old_copies = [pltpu.make_async_copy(r, grads.at[:, shard_rows(k), :], grad_sem.at[k]) for k, r in enumerate(old_refs)]
    new_copies = [pltpu.make_async_copy(grads.at[:, shard_rows(k), :], r, grad_sem.at[k]) for k, r in enumerate(grad_refs)]

    @pl.when(step == 0)
    def _():
        for copy in w_copies + old_copies:
            copy.start()
        if not carry:
            grads[...] = jnp.zeros_like(grads)
        for copy in w_copies + old_copies:
            copy.wait()

    @pl.when(step < tiles)
    def _():
        row = step * TILE + lax.broadcasted_iota(I32, (TILE, 1), 0)
        tok = jnp.where(row < total, tok_ref[...].astype(F32), 0.0).astype(BF16)
        x, dy, g = tok[:, :d_model], tok[:, d_model:2 * d_model], tok[:, 2 * d_model:]
        x_t[...] = x.T
        g_t[...] = g.T
        dx_sum[...] = jnp.zeros_like(dx_sum) if first else dx_in[...]

        def chunk(c, dg):
            cols = pl.ds(pl.multiple_of(c * CHUNK, CHUNK), CHUNK)
            w_a, w_b, w_c = w_mem[0, :, cols], w_mem[1, :, cols], w_mem[2, :, cols]
            h_one = matmul(x, w_a)
            h_three = matmul(x, w_c)
            y_part = matmul(dy, w_b)
            d_act = matmul(g, w_b)
            sigma = jax.nn.sigmoid(h_one)
            silu = h_one * sigma
            act = (silu * h_three).astype(BF16)
            prod = act.astype(F32) * y_part
            dh_three = (d_act * silu).astype(BF16)
            dh_one = (d_act * h_three * sigma * (1.0 + h_one * (1.0 - sigma))).astype(BF16)
            grads[0, :, cols] += matmul(x_t[...], dh_one)
            grads[1, :, cols] += matmul(g_t[...], act)
            grads[2, :, cols] += matmul(x_t[...], dh_three)
            dx_sum[...] += matmul_nt(dh_one, w_a) + matmul_nt(dh_three, w_c)
            for j in range(CHUNK // LANES):
                dg = dg + prod[:, j * LANES:(j + 1) * LANES]
            return dg

        dg_out[...] = lax.fori_loop(0, width // CHUNK, chunk, jnp.zeros((TILE, LANES), F32) if first else dg_in[...])
        dx_out[...] = dx_sum[...].astype(dx_out.dtype)

    @pl.when(step == pl.num_programs(0) - 1)
    def _():
        for copy in new_copies:
            copy.start()
        for copy in new_copies:
            copy.wait()


def expert_block(info, tok, w_pieces, first_col, width, partial, old, last):
    rows, d_model = tok.shape[0], tok.shape[1] // 3
    shards = len(w_pieces)
    d_shard = d_model // shards
    first, carry = partial is None, old is not None
    row_block = lambda i, info: (jnp.minimum(i, jnp.maximum(info[0] - 1, 0)), 0)
    dx_spec, dg_spec = pl.BlockSpec((TILE, d_model), row_block), pl.BlockSpec((TILE, LANES), row_block)
    ins = [tok] + list(w_pieces) + ([] if first else list(partial)) + (list(old) if carry else [])
    in_specs = [pl.BlockSpec((TILE, 3 * d_model), row_block)] + [ANY] * shards + ([] if first else [dx_spec, dg_spec]) + ([ANY] * shards if carry else [])
    grad_shape = jax.ShapeDtypeStruct((3, d_shard, width), F32)
    dx_type = BF16 if last else F32
    aliases = {}
    if not first:
        aliases[1 + 1 + shards + 1] = 1
        if not last:
            aliases[1 + 1 + shards] = 0
    outs = pl.pallas_call(
        functools.partial(expert_kernel, shards, d_model, width, first_col, first, carry),
        out_shape=[jax.ShapeDtypeStruct((rows, d_model), dx_type), jax.ShapeDtypeStruct((rows, LANES), F32)] + [grad_shape] * shards,
        grid_spec=pltpu.PrefetchScalarGridSpec(
            num_scalar_prefetch=1,
            grid=(rows // TILE,),
            in_specs=in_specs,
            out_specs=[dx_spec, dg_spec] + [ANY] * shards,
            scratch_shapes=[
                pltpu.VMEM((3, d_model, width), BF16),
                pltpu.VMEM((3, d_model, width), F32),
                pltpu.VMEM((d_model, TILE), BF16),
                pltpu.VMEM((d_model, TILE), BF16),
                pltpu.VMEM((TILE, d_model), F32),
                pltpu.SemaphoreType.DMA((shards,)),
                pltpu.SemaphoreType.DMA((shards,)),
            ],
        ),
        input_output_aliases=aliases,
        compiler_params=params(),
        cost_estimate=pl.CostEstimate(flops=18 * (rows * 6 // 10) * d_model * width, bytes_accessed=40 * 2**20, transcendentals=rows * width),
        name='expert',
    )(info, *ins)
    return outs[:2], outs[2:]


def assemble_kernel(shards, first_col, width, fresh, info, *refs):
    piece_refs = refs[:shards]
    out_refs = refs[shards + (0 if fresh else 3):][:3]
    mem, in_sem, out_sem = refs[-3:]
    my_shard = info[0]
    loads = [pltpu.make_async_copy(piece_refs[k], mem.at[k], in_sem.at[k]) for k in range(shards)]
    stores = [[pltpu.make_async_copy(mem.at[k, j], out_refs[j].at[my_shard ^ k, :, pl.ds(first_col, width)], out_sem.at[k, j]) for j in range(3)] for k in range(shards)]
    for load in loads:
        load.start()
    for k in range(shards):
        loads[k].wait()
        for store in stores[k]:
            store.start()
    for k in range(shards):
        for store in stores[k]:
            store.wait()


def assemble(info, pieces, first_col, width, ff_dim, outs):
    shards = len(pieces)
    d_shard = pieces[0].shape[1]
    fresh = outs is None
    return pl.pallas_call(
        functools.partial(assemble_kernel, shards, first_col, width, fresh),
        out_shape=[jax.ShapeDtypeStruct((shards, d_shard, ff_dim), F32)] * 3,
        in_specs=[pl.BlockSpec(memory_space=pltpu.SMEM)] + [ANY] * (shards + (0 if fresh else 3)),
        out_specs=[ANY] * 3,
        scratch_shapes=[pltpu.VMEM((shards, 3, d_shard, width), F32), pltpu.SemaphoreType.DMA((shards,)), pltpu.SemaphoreType.DMA((shards, 3))],
        input_output_aliases={} if fresh else {1 + shards + j: j for j in range(3)},
        compiler_params=params(),
        cost_estimate=pl.CostEstimate(flops=10**9, bytes_accessed=20 * 2**20, transcendentals=0),
        name='assemble',
    )(info, *pieces, *([] if fresh else outs))


def solution(mesh):
    shards, ep_size = mesh.shape['fsdp'], mesh.shape['ep']
    devices = shards * ep_size
    tok_spec = P(None, BOTH, None)
    spec_edf = P('ep', 'fsdp', None)
    spec_efd = P('ep', None, 'fsdp')

    def local_step(x_in, dy_out, expert_idx, gate_prob, w_one, w_two, w_three):
        micro, tok_rows, d_model = x_in.shape
        top_k = expert_idx.shape[2]
        local_experts, d_shard, ff_dim = w_one.shape
        assert local_experts == shards
        capacity = capacity_of(tok_rows, top_k, devices)
        n_choice = tok_rows * top_k
        slots = devices * capacity
        blk, half = ff_dim // BLOCKS, ff_dim // HALVES
        my_shard = lax.axis_index('fsdp')
        me = my_shard * ep_size + lax.axis_index('ep')
        shard_info = my_shard.astype(I32)[None]

        w_all = [w_one, jnp.swapaxes(w_two, 1, 2), w_three]

        def send_half(h):
            pieces = []
            for k in range(shards):
                cut = [lax.dynamic_slice(w, (my_shard ^ k, 0, h * half), (1, d_shard, half))[0] for w in w_all]
                pieces.append(swap(jnp.stack(cut), 'fsdp', k, shards))
            return pieces

        w_halves = [send_half(0)]

        ids = expert_idx.reshape(micro, n_choice)
        dest = ((ids % local_experts) * ep_size + ids // local_experts) ^ me
        one_hot = (dest[:, None, :] == jnp.arange(devices, dtype=I32)[None, :, None]).astype(I32)
        running = jnp.cumsum(one_hot, axis=2)
        position = jnp.sum((running - one_hot) * one_hot, axis=1)
        kept = jnp.minimum(running[:, :, -1], capacity)
        choice_slot = jnp.where(position < capacity, dest * capacity + position, slots)

        zero_row = jnp.zeros((1, 2 * d_model), x_in.dtype)
        sent_tok, sent_gate = [], []
        for m in range(micro):
            holder = jnp.full((slots + 1,), n_choice, I32).at[choice_slot[m]].set(jnp.arange(n_choice, dtype=I32))[:slots]
            table = jnp.concatenate([jnp.concatenate([x_in[m], dy_out[m]], axis=1), zero_row], axis=0)
            tok_slot = (holder // top_k).reshape(devices, capacity)
            sent_tok.append([swap(table[tok_slot[k]], BOTH, k, devices) for k in range(devices)])
            gate_pad = jnp.concatenate([gate_prob[m].reshape(n_choice), jnp.zeros((1,), F32)])
            gate_slot = gate_pad[holder].reshape(devices, capacity)
            gate_slot = jnp.concatenate([gate_slot, jnp.broadcast_to(kept[m].astype(F32)[:, None], (devices, LANES))], axis=1)
            sent_gate.append(jnp.stack([swap(gate_slot[k], BOTH, k, devices) for k in range(devices)]))
        w_halves.append(send_half(1))

        dx_parts, dg_parts = [], []
        grads = [None] * BLOCKS
        outs = None
        for m in range(micro):
            gates = sent_gate[m]
            counts = gates[:, capacity].astype(I32)
            sizes = (counts + ALIGN - 1) // ALIGN * ALIGN
            starts = jnp.cumsum(sizes) - sizes
            place = jnp.stack([starts, sizes])
            total = jnp.sum(sizes)
            info = jnp.stack([(total + TILE - 1) // TILE, total, my_shard.astype(I32)])
            gate_wide = jnp.broadcast_to(gates[:, :capacity, None], (devices, capacity, LANES))
            tok = pack(place, sent_tok[m], gate_wide, capacity, d_model)
            partial = None
            for b in range(BLOCKS):
                h, col = b * blk // half, b * blk % half
                partial, grads[b] = expert_block(info, tok, w_halves[h], col, blk, partial, grads[b], b == BLOCKS - 1)
            back = unpack(place, partial[0], devices, capacity)
            back = jnp.concatenate([swap(v, BOTH, k, devices) for k, v in enumerate(back)] + [zero_row[:, :d_model]])
            dg_rows = jnp.concatenate([jnp.sum(partial[1], axis=1), jnp.zeros((capacity,), F32)])
            dg_back = [swap(lax.dynamic_slice(dg_rows, (starts[k],), (capacity,)), BOTH, k, devices) for k in range(devices)]
            dg_back = jnp.concatenate(dg_back + [jnp.zeros((1,), F32)])
            slot = choice_slot[m].reshape(tok_rows, top_k)
            total_dx = sum(back[slot[:, j]].astype(F32) for j in range(top_k))
            dx_parts.append(total_dx.astype(BF16))
            dg_parts.append(dg_back[choice_slot[m]].reshape(tok_rows, top_k))
        for b in range(BLOCKS):
            moved = [swap(v, 'fsdp', k, shards) for k, v in enumerate(grads[b])]
            outs = assemble(shard_info, moved, b * blk, blk, ff_dim, outs)
        dw_one, dw_two, dw_three = outs
        return jnp.stack(dx_parts), jnp.stack(dg_parts), dw_one, jnp.swapaxes(dw_two, 1, 2), dw_three

    return jax.shard_map(local_step, mesh=mesh, in_specs=(tok_spec, tok_spec, tok_spec, tok_spec, spec_edf, spec_efd, spec_edf), out_specs=(tok_spec, tok_spec, spec_edf, spec_efd, spec_edf), check_vma=False)
```

profile of v0, /device:TPU:0, one launch (start us, length us, event | category | flops | bytes accessed | tf_op | source)
XLA Modules:
  0.0 2032.5 jit_solution(14061150102747135154)
XLA Ops:
  27.5 28.7 %gather_fusion = f32[5120]{0:T(1024)S(1)} fusion(f32[4097]{0:T(1024)S(1)} %pad_maximum_fusion.11, s32[5120]{0:T(1024)S(1)} %get-tuple-element.226), kind=kCustom, calls=%fused_computation | custom fusion | bytes 61440 | tf_op jit(solution)/shard_map/gather | solution.py:334
  122.5 28.6 %gather_fusion.11 = f32[5120]{0:T(1024)S(1)} fusion(f32[4097]{0:T(1024)S(1)} %pad_maximum_fusion.10, s32[5120]{0:T(1024)S(1)} %get-tuple-element.231), kind=kCustom, calls=%fused_computation.11 | custom fusion | bytes 61440 | tf_op jit(solution)/shard_map/gather | solution.py:334
  304.3 62.1 %collective-permute-done.11.refs_5_ = bf16[640,1536]{1,0:T(8,128)(2,1)} collective-permute-done((bf16[640,1536]{1,0:T(8,128)(2,1)}, bf16[640,1536]{1,0:T(8,128)(2,1)}, u32[]{:S(2)}, u32[]{:S(2)}) %collective-permute-start.11) | collective-permute-done | bytes 1966112 | tf_op jit(solution)/shard_map/ppermute | solution.py:31
  379.8 27.8 %collective-permute-done.35.refs_2_ = bf16[640,1536]{1,0:T(8,128)(2,1)S(1)} collective-permute-done((bf16[640,1536]{1,0:T(8,128)(2,1)}, bf16[640,1536]{1,0:T(8,128)(2,1)S(1)}, u32[]{:S(2)}, u32[]{:S(2)}) %collective-permute-start.35) | collective-permute-done | bytes 1966112 | tf_op jit(solution)/shard_map/ppermute | solution.py:31
  410.2 37.7 %collective-permute-done.36.refs_3_ = bf16[640,1536]{1,0:T(8,128)(2,1)S(1)} collective-permute-done((bf16[640,1536]{1,0:T(8,128)(2,1)S(1)}, bf16[640,1536]{1,0:T(8,128)(2,1)S(1)}, u32[]{:S(2)}, u32[]{:S(2)}) %collective-permute-start.36) | collective-permute-done | bytes 1966112 | tf_op jit(solution)/shard_map/ppermute | solution.py:31
  513.6 82.8 %collective-permute-done.38.refs_5_ = bf16[640,1536]{1,0:T(8,128)(2,1)} collective-permute-done((bf16[640,1536]{1,0:T(8,128)(2,1)}, bf16[640,1536]{1,0:T(8,128)(2,1)}, u32[]{:S(2)}, u32[]{:S(2)}) %collective-permute-start.38) | collective-permute-done | bytes 1966112 | tf_op jit(solution)/shard_map/ppermute | solution.py:31
  614.1 67.5 %expert.8 = (f32[5120,768]{1,0:T(8,128)}, f32[5120,128]{1,0:T(8,128)}, f32[3,192,1024]{2,1,0:T(8,128)}, f32[3,192,1024]{2,1,0:T(8,128)}, f32[3,192,1024]{2,1,0:T(8,128)}, /*index=5*/f32[3,192,1024]{2,1,0:T(8,128)}) custom-call(s32[3]{0:T(128)} %add_add_fusion.info, bf16[5120,2304]{1,0:T(8,128)(2,1)} %pack.2.refs_0_, ...), custom_call_target="tpu_custom_call" | custom-call | flops 43486543872 | bytes 41943040 | tf_op jit(solution)/shard_map/expert/pallas_call | solution.py:226
  681.6 68.4 %expert.9 = (f32[5120,768]{1,0:T(8,128)}, f32[5120,128]{1,0:T(8,128)}, f32[3,192,1024]{2,1,0:T(8,128)}, f32[3,192,1024]{2,1,0:T(8,128)}, f32[3,192,1024]{2,1,0:T(8,128)}, /*index=5*/f32[3,192,1024]{2,1,0:T(8,128)}) custom-call(s32[3]{0:T(128)} %add_add_fusion.info, bf16[5120,2304]{1,0:T(8,128)(2,1)} %pack.2.refs_0_, ...), custom_call_target="tpu_custom_call", output_to_operand_aliasing={{1}: (7, {}), {0}: (6, {})} | custom-call | flops 43486543872 | bytes 41943040 | tf_op jit(solution)/shard_map/expert/pallas_call | solution.py:226
  750.0 68.5 %expert.10 = (f32[5120,768]{1,0:T(8,128)}, f32[5120,128]{1,0:T(8,128)}, f32[3,192,1024]{2,1,0:T(8,128)}, f32[3,192,1024]{2,1,0:T(8,128)}, f32[3,192,1024]{2,1,0:T(8,128)}, /*index=5*/f32[3,192,1024]{2,1,0:T(8,128)}) custom-call(s32[3]{0:T(128)} %add_add_fusion.info, bf16[5120,2304]{1,0:T(8,128)(2,1)} %pack.2.refs_0_, ...), custom_call_target="tpu_custom_call", output_to_operand_aliasing={{1}: (7, {}), {0}: (6, {})} | custom-call | flops 43486543872 | bytes 41943040 | tf_op jit(solution)/shard_map/expert/pallas_call | solution.py:226
  818.5 68.5 %expert.11 = (bf16[5120,768]{1,0:T(8,128)(2,1)}, f32[5120,128]{1,0:T(8,128)}, f32[3,192,1024]{2,1,0:T(8,128)}, f32[3,192,1024]{2,1,0:T(8,128)}, f32[3,192,1024]{2,1,0:T(8,128)}, /*index=5*/f32[3,192,1024]{2,1,0:T(8,128)}) custom-call(s32[3]{0:T(128)} %add_add_fusion.info, bf16[5120,2304]{1,0:T(8,128)(2,1)} %pack.2.refs_0_, ...), custom_call_target="tpu_custom_call", output_to_operand_aliasing={{1}: (7, {})} | custom-call | flops 43486543872 | bytes 41943040 | tf_op jit(solution)/shard_map/expert/pallas_call | solution.py:226
  895.4 41.2 %collective-permute-start.48 = (f32[640]{0:T(1024)S(1)}, f32[640]{0:T(1024)S(1)}, u32[]{:S(2)}, u32[]{:S(2)}) collective-permute-start(f32[640]{0:T(1024)S(1)} %get-tuple-element.236), channel_id=1, source_target_pairs={{0,1},{1,0},{2,3},{3,2},{4,5},{5,4},{6,7},{7,6}} | collective-permute-start | bytes 7688 | tf_op jit(solution)/shard_map/ppermute | solution.py:31
  938.7 98.7 %expert.12 = (f32[5120,768]{1,0:T(8,128)}, f32[5120,128]{1,0:T(8,128)}, f32[3,192,1024]{2,1,0:T(8,128)}, f32[3,192,1024]{2,1,0:T(8,128)}, f32[3,192,1024]{2,1,0:T(8,128)}, /*index=5*/f32[3,192,1024]{2,1,0:T(8,128)}) custom-call(s32[3]{0:T(128)} %add_add_fusion.1.info, bf16[5120,2304]{1,0:T(8,128)(2,1)} %pack.3.refs_0_, ...), custom_call_target="tpu_custom_call" | custom-call | flops 43486543872 | bytes 41943040 | tf_op jit(solution)/shard_map/expert/pallas_call | solution.py:226
  1037.5 100.0 %expert.13 = (f32[5120,768]{1,0:T(8,128)}, f32[5120,128]{1,0:T(8,128)}, f32[3,192,1024]{2,1,0:T(8,128)}, f32[3,192,1024]{2,1,0:T(8,128)}, f32[3,192,1024]{2,1,0:T(8,128)}, /*index=5*/f32[3,192,1024]{2,1,0:T(8,128)}) custom-call(s32[3]{0:T(128)} %add_add_fusion.1.info, bf16[5120,2304]{1,0:T(8,128)(2,1)} %pack.3.refs_0_, ...), custom_call_target="tpu_custom_call", output_to_operand_aliasing={{1}: (7, {}), {0}: (6, {})} | custom-call | flops 43486543872 | bytes 41943040 | tf_op jit(solution)/shard_map/expert/pallas_call | solution.py:226
  1137.5 100.3 %expert.14 = (f32[5120,768]{1,0:T(8,128)}, f32[5120,128]{1,0:T(8,128)}, f32[3,192,1024]{2,1,0:T(8,128)}, f32[3,192,1024]{2,1,0:T(8,128)}, f32[3,192,1024]{2,1,0:T(8,128)}, /*index=5*/f32[3,192,1024]{2,1,0:T(8,128)}) custom-call(s32[3]{0:T(128)} %add_add_fusion.1.info, bf16[5120,2304]{1,0:T(8,128)(2,1)} %pack.3.refs_0_, ...), custom_call_target="tpu_custom_call", output_to_operand_aliasing={{1}: (7, {}), {0}: (6, {})} | custom-call | flops 43486543872 | bytes 41943040 | tf_op jit(solution)/shard_map/expert/pallas_call | solution.py:226
  1237.9 99.4 %expert.15 = (bf16[5120,768]{1,0:T(8,128)(2,1)}, f32[5120,128]{1,0:T(8,128)}, f32[3,192,1024]{2,1,0:T(8,128)}, f32[3,192,1024]{2,1,0:T(8,128)}, f32[3,192,1024]{2,1,0:T(8,128)}, /*index=5*/f32[3,192,1024]{2,1,0:T(8,128)}) custom-call(s32[3]{0:T(128)} %add_add_fusion.1.info, bf16[5120,2304]{1,0:T(8,128)(2,1)} %pack.3.refs_0_, ...), custom_call_target="tpu_custom_call", output_to_operand_aliasing={{1}: (7, {})} | custom-call | flops 43486543872 | bytes 41943040 | tf_op jit(solution)/shard_map/expert/pallas_call | solution.py:226
  1370.7 55.1 %collective-permute-done.23 = bf16[640,768]{1,0:T(8,128)(2,1)S(1)} collective-permute-done((bf16[640,768]{1,0:T(8,128)(2,1)}, bf16[640,768]{1,0:T(8,128)(2,1)S(1)}, u32[]{:S(2)}, u32[]{:S(2)}) %collective-permute-start.23) | collective-permute-done | bytes 983072 | tf_op jit(solution)/shard_map/ppermute | solution.py:31
  1453.9 98.9 %collective-permute-done.42 = bf16[640,768]{1,0:T(8,128)(2,1)} collective-permute-done((bf16[640,768]{1,0:T(8,128)(2,1)}, bf16[640,768]{1,0:T(8,128)(2,1)}, u32[]{:S(2)}, u32[]{:S(2)}) %collective-permute-start.42) | collective-permute-done | bytes 983072 | tf_op jit(solution)/shard_map/ppermute | solution.py:31
  1571.9 45.6 %collective-permute-done.45 = bf16[640,768]{1,0:T(8,128)(2,1)S(1)} collective-permute-done((bf16[640,768]{1,0:T(8,128)(2,1)S(1)}, bf16[640,768]{1,0:T(8,128)(2,1)S(1)}, u32[]{:S(2)}, u32[]{:S(2)}) %collective-permute-start.45) | collective-permute-done | bytes 983072 | tf_op jit(solution)/shard_map/ppermute | solution.py:31
  1623.7 23.2 %gather_fusion.22 = f32[4096]{0:T(1024)S(1)} fusion(f32[5121]{0:T(1024)S(1)} %constant_dynamic-update-slice_fusion.34, s32[4096]{0:T(1024)S(1)} %broadcast_clamp_fusion.1), kind=kCustom, calls=%fused_computation.22 | custom fusion | bytes 49152 | tf_op jit(solution)/shard_map/gather | solution.py:364
  1648.4 23.0 %gather_fusion.23 = f32[4096]{0:T(1024)S(1)} fusion(f32[5121]{0:T(1024)S(1)} %constant_dynamic-update-slice_fusion.35, s32[4096]{0:T(1024)S(1)} %broadcast_clamp_fusion), kind=kCustom, calls=%fused_computation.23 | custom fusion | bytes 49152 | tf_op jit(solution)/shard_map/gather | solution.py:364
  1694.2 28.3 %collective-permute-done.69.refs_2_ = f32[3,192,1024]{2,1,0:T(8,128)} collective-permute-done((f32[3,192,1024]{2,1,0:T(8,128)}, f32[3,192,1024]{2,1,0:T(8,128)}, u32[]{:S(2)}, u32[]{:S(2)}) %collective-permute-start.69) | collective-permute-done | bytes 2359328 | tf_op jit(solution)/shard_map/ppermute | solution.py:31
  1754.2 120.0 %collective-permute-done.72.refs_2_ = f32[3,192,1024]{2,1,0:T(8,128)} collective-permute-done((f32[3,192,1024]{2,1,0:T(8,128)}, f32[3,192,1024]{2,1,0:T(8,128)}, u32[]{:S(2)}, u32[]{:S(2)}) %collective-permute-start.72) | collective-permute-done | bytes 2359328 | tf_op jit(solution)/shard_map/ppermute | solution.py:31
  1933.1 42.2 %collective-permute-done.66.refs_2_ = f32[3,192,1024]{2,1,0:T(8,128)} collective-permute-done((f32[3,192,1024]{2,1,0:T(8,128)}, f32[3,192,1024]{2,1,0:T(8,128)}, u32[]{:S(2)}, u32[]{:S(2)}) %collective-permute-start.66) | collective-permute-done | bytes 2359328 | tf_op jit(solution)/shard_map/ppermute | solution.py:31
  1983.2 41.3 %collective-permute-done.63.refs_2_ = f32[3,192,1024]{2,1,0:T(8,128)} collective-permute-done((f32[3,192,1024]{2,1,0:T(8,128)}, f32[3,192,1024]{2,1,0:T(8,128)}, u32[]{:S(2)}, u32[]{:S(2)}) %collective-permute-start.63) | collective-permute-done | bytes 2359328 | tf_op jit(solution)/shard_map/ppermute | solution.py:31
  (437 shorter events, 540.6 us)
Async XLA Ops:
  223.9 142.5 %collective-permute-start.11 = (bf16[640,1536]{1,0:T(8,128)(2,1)}, bf16[640,1536]{1,0:T(8,128)(2,1)}, u32[]{:S(2)}, u32[]{:S(2)}) collective-permute-start(bf16[640,1536]{1,0:T(8,128)(2,1)} %gather_fusion.6), channel_id=1, source_target_pairs={{0,5},{1,4},{2,7},{3,6},{4,1},{5,0},{6,3},{7,2}} | collective-permute-start | bytes 5898248 | tf_op jit(solution)/shard_map/ppermute | solution.py:31
  225.0 142.0 %collective-permute-start.12 = (bf16[640,1536]{1,0:T(8,128)(2,1)}, bf16[640,1536]{1,0:T(8,128)(2,1)}, u32[]{:S(2)}, u32[]{:S(2)}) collective-permute-start(bf16[640,1536]{1,0:T(8,128)(2,1)} %gather_fusion.7), channel_id=1, source_target_pairs={{0,6},{1,7},{2,4},{3,5},{4,2},{5,3},{6,0},{7,1}} | collective-permute-start | bytes 5898248 | tf_op jit(solution)/shard_map/ppermute | solution.py:31
  377.8 236.2 %collective-permute-start.18 = (bf16[3,192,2048]{2,1,0:T(8,128)(2,1)}, bf16[3,192,2048]{2,1,0:T(8,128)(2,1)}, u32[]{:S(2)}, u32[]{:S(2)}) collective-permute-start(bf16[3,192,2048]{2,1,0:T(8,128)(2,1)} %pad_maximum_fusion.7), channel_id=1, source_target_pairs={{0,4},{2,6},{4,0},{6,2},{1,5},{3,7},{5,1},{7,3}} | collective-permute-start | bytes 7077896 | tf_op jit(solution)/shard_map/ppermute | solution.py:31
  378.9 235.1 %collective-permute-start.17 = (bf16[3,192,2048]{2,1,0:T(8,128)(2,1)}, bf16[3,192,2048]{2,1,0:T(8,128)(2,1)}, u32[]{:S(2)}, u32[]{:S(2)}) collective-permute-start(bf16[3,192,2048]{2,1,0:T(8,128)(2,1)} %pad_maximum_fusion.6), channel_id=1, source_target_pairs={{0,2},{2,0},{4,6},{6,4},{1,3},{3,1},{5,7},{7,5}} | collective-permute-start | bytes 7077896 | tf_op jit(solution)/shard_map/ppermute | solution.py:31
  407.6 206.5 %collective-permute-start.19 = (bf16[3,192,2048]{2,1,0:T(8,128)(2,1)S(1)}, bf16[3,192,2048]{2,1,0:T(8,128)(2,1)}, u32[]{:S(2)}, u32[]{:S(2)}) collective-permute-start(bf16[3,192,2048]{2,1,0:T(8,128)(2,1)S(1)} %pad_maximum_fusion.8), channel_id=1, source_target_pairs={{0,6},{2,4},{4,2},{6,0},{1,7},{3,5},{5,3},{7,1}} | collective-permute-start | bytes 7077896 | tf_op jit(solution)/shard_map/ppermute | solution.py:31
  447.9 148.4 %collective-permute-start.38 = (bf16[640,1536]{1,0:T(8,128)(2,1)}, bf16[640,1536]{1,0:T(8,128)(2,1)}, u32[]{:S(2)}, u32[]{:S(2)}) collective-permute-start(bf16[640,1536]{1,0:T(8,128)(2,1)} %gather_fusion.17), channel_id=1, source_target_pairs={{0,5},{1,4},{2,7},{3,6},{4,1},{5,0},{6,3},{7,2}} | collective-permute-start | bytes 5898248 | tf_op jit(solution)/shard_map/ppermute | solution.py:31
  450.5 148.0 %collective-permute-start.39 = (bf16[640,1536]{1,0:T(8,128)(2,1)}, bf16[640,1536]{1,0:T(8,128)(2,1)}, u32[]{:S(2)}, u32[]{:S(2)}) collective-permute-start(bf16[640,1536]{1,0:T(8,128)(2,1)} %gather_fusion.18), channel_id=1, source_target_pairs={{0,6},{1,7},{2,4},{3,5},{4,2},{5,3},{6,0},{7,1}} | collective-permute-start | bytes 5898248 | tf_op jit(solution)/shard_map/ppermute | solution.py:31
  596.3 153.7 %collective-permute-start.14 = (bf16[3,192,2048]{2,1,0:T(8,128)(2,1)}, bf16[3,192,2048]{2,1,0:T(8,128)(2,1)}, u32[]{:S(2)}, u32[]{:S(2)}) collective-permute-start(bf16[3,192,2048]{2,1,0:T(8,128)(2,1)} %pad_maximum_fusion.2), channel_id=1, source_target_pairs={{0,2},{2,0},{4,6},{6,4},{1,3},{3,1},{5,7},{7,5}} | collective-permute-start | bytes 7077896 | tf_op jit(solution)/shard_map/ppermute | solution.py:31
  598.5 151.5 %collective-permute-start.15 = (bf16[3,192,2048]{2,1,0:T(8,128)(2,1)}, bf16[3,192,2048]{2,1,0:T(8,128)(2,1)}, u32[]{:S(2)}, u32[]{:S(2)}) collective-permute-start(bf16[3,192,2048]{2,1,0:T(8,128)(2,1)} %pad_maximum_fusion.3), channel_id=1, source_target_pairs={{0,4},{2,6},{4,0},{6,2},{1,5},{3,7},{5,1},{7,3}} | collective-permute-start | bytes 7077896 | tf_op jit(solution)/shard_map/ppermute | solution.py:31
  614.0 136.0 %collective-permute-start.16 = (bf16[3,192,2048]{2,1,0:T(8,128)(2,1)}, bf16[3,192,2048]{2,1,0:T(8,128)(2,1)}, u32[]{:S(2)}, u32[]{:S(2)}) collective-permute-start(bf16[3,192,2048]{2,1,0:T(8,128)(2,1)} %pad_maximum_fusion.4), channel_id=1, source_target_pairs={{0,6},{2,4},{4,2},{6,0},{1,7},{3,5},{5,3},{7,1}} | collective-permute-start | bytes 7077896 | tf_op jit(solution)/shard_map/ppermute | solution.py:31
  895.4 342.4 %collective-permute-start.54 = (f32[640]{0:T(1024)S(1)}, f32[640]{0:T(1024)S(1)}, u32[]{:S(2)}, u32[]{:S(2)}) collective-permute-start(f32[640]{0:T(1024)S(1)} %get-tuple-element.235), channel_id=1, source_target_pairs={{0,7},{1,6},{2,5},{3,4},{4,3},{5,2},{6,1},{7,0}} | collective-permute-start | bytes 7688 | tf_op jit(solution)/shard_map/ppermute | solution.py:31
  895.4 342.5 %collective-permute-start.48 = (f32[640]{0:T(1024)S(1)}, f32[640]{0:T(1024)S(1)}, u32[]{:S(2)}, u32[]{:S(2)}) collective-permute-start(f32[640]{0:T(1024)S(1)} %get-tuple-element.236), channel_id=1, source_target_pairs={{0,1},{1,0},{2,3},{3,2},{4,5},{5,4},{6,7},{7,6}} | collective-permute-start | bytes 7688 | tf_op jit(solution)/shard_map/ppermute | solution.py:31
  936.6 403.2 %collective-permute-start.49 = (f32[640]{0:T(1024)}, f32[640]{0:T(1024)}, u32[]{:S(2)}, u32[]{:S(2)}) collective-permute-start(f32[640]{0:T(1024)} %get-tuple-element.237), channel_id=1, source_target_pairs={{0,2},{1,3},{2,0},{3,1},{4,6},{5,7},{6,4},{7,5}} | collective-permute-start | bytes 7688 | tf_op jit(solution)/shard_map/ppermute | solution.py:31
  936.6 403.3 %collective-permute-start.50 = (f32[640]{0:T(1024)}, f32[640]{0:T(1024)}, u32[]{:S(2)}, u32[]{:S(2)}) collective-permute-start(f32[640]{0:T(1024)} %get-tuple-element.238), channel_id=1, source_target_pairs={{0,3},{1,2},{2,1},{3,0},{4,7},{5,6},{6,5},{7,4}} | collective-permute-start | bytes 7688 | tf_op jit(solution)/shard_map/ppermute | solution.py:31
  938.0 421.8 %collective-permute-start.20 = (bf16[640,768]{1,0:T(8,128)(2,1)}, bf16[640,768]{1,0:T(8,128)(2,1)}, u32[]{:S(2)}, u32[]{:S(2)}) collective-permute-start(bf16[640,768]{1,0:T(8,128)(2,1)} %get-tuple-element.89), channel_id=1, source_target_pairs={{0,1},{1,0},{2,3},{3,2},{4,5},{5,4},{6,7},{7,6}} | collective-permute-start | bytes 2949128 | tf_op jit(solution)/shard_map/ppermute | solution.py:31
  1426.7 194.4 %collective-permute-start.65 = (f32[3,192,1024]{2,1,0:T(8,128)}, f32[3,192,1024]{2,1,0:T(8,128)S(1)}, u32[]{:S(2)}, u32[]{:S(2)}) collective-permute-start(f32[3,192,1024]{2,1,0:T(8,128)} %get-tuple-element.134), channel_id=1, source_target_pairs={{0,2},{2,0},{4,6},{6,4},{1,3},{3,1},{5,7},{7,5}} | collective-permute-start | bytes 7077896 | tf_op jit(solution)/shard_map/ppermute | solution.py:31
  1442.1 179.8 %collective-permute-start.68 = (f32[3,192,1024]{2,1,0:T(8,128)}, f32[3,192,1024]{2,1,0:T(8,128)}, u32[]{:S(2)}, u32[]{:S(2)}) collective-permute-start(f32[3,192,1024]{2,1,0:T(8,128)} %get-tuple-element.138), channel_id=1, source_target_pairs={{0,2},{2,0},{4,6},{6,4},{1,3},{3,1},{5,7},{7,5}} | collective-permute-start | bytes 7077896 | tf_op jit(solution)/shard_map/ppermute | solution.py:31
  1621.1 253.1 %collective-permute-start.72 = (f32[3,192,1024]{2,1,0:T(8,128)}, f32[3,192,1024]{2,1,0:T(8,128)}, u32[]{:S(2)}, u32[]{:S(2)}) collective-permute-start(f32[3,192,1024]{2,1,0:T(8,128)} %get-tuple-element.143), channel_id=1, source_target_pairs={{0,4},{2,6},{4,0},{6,2},{1,5},{3,7},{5,1},{7,3}} | collective-permute-start | bytes 7077896 | tf_op jit(solution)/shard_map/ppermute | solution.py:31
  1621.9 253.1 %collective-permute-start.73 = (f32[3,192,1024]{2,1,0:T(8,128)}, f32[3,192,1024]{2,1,0:T(8,128)}, u32[]{:S(2)}, u32[]{:S(2)}) collective-permute-start(f32[3,192,1024]{2,1,0:T(8,128)} %get-tuple-element.144), channel_id=1, source_target_pairs={{0,6},{2,4},{4,2},{6,0},{1,7},{3,5},{5,3},{7,1}} | collective-permute-start | bytes 7077896 | tf_op jit(solution)/shard_map/ppermute | solution.py:31
  1722.5 252.8 %collective-permute-start.66 = (f32[3,192,1024]{2,1,0:T(8,128)}, f32[3,192,1024]{2,1,0:T(8,128)}, u32[]{:S(2)}, u32[]{:S(2)}) collective-permute-start(f32[3,192,1024]{2,1,0:T(8,128)} %get-tuple-element.135), channel_id=1, source_target_pairs={{0,4},{2,6},{4,0},{6,2},{1,5},{3,7},{5,1},{7,3}} | collective-permute-start | bytes 7077896 | tf_op jit(solution)/shard_map/ppermute | solution.py:31
  1724.6 250.7 %collective-permute-start.67 = (f32[3,192,1024]{2,1,0:T(8,128)}, f32[3,192,1024]{2,1,0:T(8,128)}, u32[]{:S(2)}, u32[]{:S(2)}) collective-permute-start(f32[3,192,1024]{2,1,0:T(8,128)} %get-tuple-element.136), channel_id=1, source_target_pairs={{0,6},{2,4},{4,2},{6,0},{1,7},{3,5},{5,3},{7,1}} | collective-permute-start | bytes 7077896 | tf_op jit(solution)/shard_map/ppermute | solution.py:31
  1754.2 229.0 %collective-permute-start.62 = (f32[3,192,1024]{2,1,0:T(8,128)}, f32[3,192,1024]{2,1,0:T(8,128)}, u32[]{:S(2)}, u32[]{:S(2)}) collective-permute-start(f32[3,192,1024]{2,1,0:T(8,128)} %get-tuple-element.130), channel_id=1, source_target_pairs={{0,2},{2,0},{4,6},{6,4},{1,3},{3,1},{5,7},{7,5}} | collective-permute-start | bytes 7077896 | tf_op jit(solution)/shard_map/ppermute | solution.py:31
  1874.2 150.2 %collective-permute-start.63 = (f32[3,192,1024]{2,1,0:T(8,128)}, f32[3,192,1024]{2,1,0:T(8,128)}, u32[]{:S(2)}, u32[]{:S(2)}) collective-permute-start(f32[3,192,1024]{2,1,0:T(8,128)} %get-tuple-element.131), channel_id=1, source_target_pairs={{0,4},{2,6},{4,0},{6,2},{1,5},{3,7},{5,1},{7,3}} | collective-permute-start | bytes 7077896 | tf_op jit(solution)/shard_map/ppermute | solution.py:31
  1875.1 149.4 %collective-permute-start.64 = (f32[3,192,1024]{2,1,0:T(8,128)}, f32[3,192,1024]{2,1,0:T(8,128)}, u32[]{:S(2)}, u32[]{:S(2)}) collective-permute-start(f32[3,192,1024]{2,1,0:T(8,128)} %get-tuple-element.132), channel_id=1, source_target_pairs={{0,6},{2,4},{4,2},{6,0},{1,7},{3,5},{5,3},{7,1}} | collective-permute-start | bytes 7077896 | tf_op jit(solution)/shard_map/ppermute | solution.py:31
  (108 other events, 5100.2 us)
where the time goes:
time: 2040 us; the launch traced here: 2030 us
  Pallas kernels  740 us (36%)
  waiting for transfers between devices  686 us (34%)
  local copies, waits for them, and re-layouts  413 us (20%)
  starting transfers between devices  111 us (5%)
  other arithmetic  48.1 us (2%)
  between operations  34.3 us (2%)
    ppermute x74, waiting for transfers between devices, swap(): return lax.ppermute(value, axes, [(s, s ^ shift) for s in range(devices)])  686 us
    pallas_call x8, Pallas kernels, expert_block(): pl.pallas_call(functools.partial(expert_kernel, shards, d_model, width, f...  671 us
    gather x16, local copies, waits for them, and re-layouts, local_step(): table[tok_slot[k]]  151 us
    ppermute x74, starting transfers between devices, swap(): return lax.ppermute(value, axes, [(s, s ^ shift) for s in range(devices)])  111 us
    gather x2, local copies, waits for them, and re-layouts, local_step(): gate_slot = gate_pad[holder].reshape(devices, capacity)  57.3 us
    gather x4, local copies, waits for them, and re-layouts, local_step(): total_dx = sum((back[slot[:, j]].astype(F32) for j in range(top_k)))  55.9 us
    gather x2, local copies, waits for them, and re-layouts, local_step(): dg_parts.append(dg_back[choice_slot[m]].reshape(tok_rows, top_k))  46.3 us
  transfers between devices with their start and end apart: 74, of which 23 were waited for; matrix products, arithmetic and copies ran while one was open for 20% of the time, Pallas kernels for 29%

commit v1 on v0

v1 whole, which is shorter than its diff:
```python
import functools

import jax
import jax.numpy as jnp
from jax import lax
from jax.experimental import pallas as pl
from jax.experimental.pallas import tpu as pltpu
from jax.sharding import PartitionSpec as P


BLOCKS = 4
TILE = 512
CHUNK = 256
ALIGN = 16
LANES = 128
BF16 = jnp.bfloat16
F32 = jnp.float32
I32 = jnp.int32
BOTH = ('fsdp', 'ep')
ANY = pl.BlockSpec(memory_space=pl.ANY)


def capacity_of(tok_rows, top_k, experts):
    return 8 * ((5 * tok_rows * top_k + 32 * experts - 1) // (32 * experts))


def swap(value, axes, shift, devices):
    if shift == 0:
        return value
    return lax.ppermute(value, axes, [(s, s ^ shift) for s in range(devices)])


def matmul(left, right):
    return jnp.dot(left, right, preferred_element_type=F32)


def matmul_nt(left, right):
    return lax.dot_general(left, right, (((1,), (1,)), ((), ())), preferred_element_type=F32)


def params():
    return pltpu.CompilerParams(vmem_limit_bytes=60 * 2**20)


def dispatch_kernel(pieces, local_experts, ep_size, capacity, micro_index, info, ids_ref, gate_ref, x_hbm, dy_hbm, *refs):
    out_refs, gates_out, slot_out = refs[:pieces], refs[pieces], refs[pieces + 1]
    table, held, held_gate, rows, table_sem, row_sem = refs[pieces + 2:]
    tokens, d_model = x_hbm.shape[1:]
    copies = [pltpu.make_async_copy(r.at[micro_index], table.at[:, pl.ds(j * d_model, d_model)], table_sem.at[j]) for j, r in enumerate((x_hbm, dy_hbm))]
    for copy in copies:
        copy.start()

    ids = ids_ref[...]
    dest = ((ids % local_experts) * ep_size + ids // local_experts) ^ info[0]
    piece = lax.broadcasted_iota(I32, (pieces, tokens), 0)
    lane = lax.broadcasted_iota(I32, (pieces, tokens), 1)
    first, second = dest[0:1] == piece, dest[1:2] == piece
    member = (first | second).astype(I32)
    running = member
    step = 1
    while step < tokens:
        running = running + jnp.where(lane >= step, pltpu.roll(running, step, 1), 0)
        step *= 2
    position = running - member
    kept = position < capacity
    held[...] = jnp.where((first | second) & kept, position, -1)
    held_gate[...] = jnp.where(first, gate_ref[0:1], gate_ref[1:2])
    slot = jnp.where(kept, piece * capacity + position, pieces * capacity)
    slot_out[0:1, :] = jnp.sum(jnp.where(first, slot, 0), axis=0, keepdims=True)
    slot_out[1:2, :] = jnp.sum(jnp.where(second, slot, 0), axis=0, keepdims=True)
    count = jnp.minimum(jnp.max(running, axis=1, keepdims=True), capacity)
    gates_out[:, pl.ds(capacity, LANES)] = jnp.broadcast_to(count.astype(F32), (pieces, LANES))
    for copy in copies:
        copy.wait()

    part = capacity // 2

    def store(k, ref):
        return pltpu.make_async_copy(rows.at[k % 2], ref, row_sem.at[k % 2])

    def one_piece(k, carry):
        @pl.when(k >= 2)
        def _():
            store(k, out_refs[0]).wait()

        wanted = held[pl.ds(k, 1), :]
        gate_row = held_gate[pl.ds(k, 1), :]
        for h in range(2):
            def half():
                place = h * part + lax.broadcasted_iota(I32, (part, LANES), 0)
                total = jnp.zeros((part, LANES), F32)
                chosen = []
                for c in range(tokens // LANES):
                    cols = slice(c * LANES, (c + 1) * LANES)
                    hit = place == wanted[:, cols]
                    total = total + jnp.where(hit, gate_row[:, cols], 0.0)
                    chosen.append(jnp.where(hit, 1.0, 0.0).astype(BF16))
                picked = matmul(jnp.concatenate(chosen, axis=1), table[...])
                rows[k % 2, pl.ds(h * part, part), :] = picked.astype(BF16)
                held_gate_row = jnp.sum(total.T, axis=0, keepdims=True)
                return held_gate_row

            used = jnp.max(wanted) >= h * part
            if h == 0:
                low = half()
            else:
                high = lax.cond(used, half, lambda: jnp.zeros((1, part), F32))
        gates_out[pl.ds(k, 1), pl.ds(0, capacity)] = jnp.concatenate([low, high], axis=1)
        for j in range(pieces):
            @pl.when(k == j)
            def _():
                store(k, out_refs[j]).start()
        return carry

    lax.fori_loop(0, pieces, one_piece, 0)
    for k in range(pieces - 2, pieces):
        store(k, out_refs[0]).wait()


def dispatch(info, ids, gates, x_in, dy_out, micro_index, pieces, local_experts, ep_size, capacity):
    tokens, d_model = x_in.shape[1:]
    vmem = pl.BlockSpec(memory_space=pltpu.VMEM)
    outs = pl.pallas_call(
        functools.partial(dispatch_kernel, pieces, local_experts, ep_size, capacity, micro_index),
        out_shape=[jax.ShapeDtypeStruct((capacity, 2 * d_model), BF16)] * pieces + [jax.ShapeDtypeStruct((pieces, capacity + LANES), F32), jax.ShapeDtypeStruct(ids.shape, I32)],
        in_specs=[pl.BlockSpec(memory_space=pltpu.SMEM), vmem, vmem, ANY, ANY],
        out_specs=[ANY] * pieces + [vmem, vmem],
        scratch_shapes=[
            pltpu.VMEM((tokens, 2 * d_model), BF16),
            pltpu.VMEM((pieces, tokens), I32),
            pltpu.VMEM((pieces, tokens), F32),
            pltpu.VMEM((2, capacity, 2 * d_model), BF16),
            pltpu.SemaphoreType.DMA((2,)),
            pltpu.SemaphoreType.DMA((2,)),
        ],
        compiler_params=params(),
        cost_estimate=pl.CostEstimate(flops=2 * pieces * capacity * tokens * 2 * d_model, bytes_accessed=24 * 2**20, transcendentals=0),
        name='dispatch',
    )(info, ids, gates, x_in, dy_out)
    return outs[:pieces], outs[pieces], outs[pieces + 1]


def pack_kernel(pieces, d_model, counts, *refs):
    tok_refs, gates_ref, out_ref, place = refs[:pieces], refs[pieces], refs[pieces + 1], refs[pieces + 2]
    tok, gates, gated, blank, in_sem, gate_sem, out_sem, blank_sem = refs[pieces + 3:]
    gate_copy = pltpu.make_async_copy(gates_ref, gates, gate_sem)
    gate_copy.start()
    loads = [pltpu.make_async_copy(tok_refs[k], tok.at[k], in_sem.at[k]) for k in range(pieces)]
    for load in loads:
        load.start()
    total = jnp.int32(0)
    for k in range(pieces):
        size = (counts[k] + ALIGN - 1) // ALIGN * ALIGN
        place[0, k], place[1, k] = total, size
        total = total + size
    tiles = (total + TILE - 1) // TILE
    place[2, 0], place[2, 1] = tiles, total
    rest = tiles * TILE - total
    blank[...] = jnp.zeros_like(blank)

    def blank_copy():
        size = pl.multiple_of(rest, ALIGN)
        return pltpu.make_async_copy(blank.at[pl.ds(0, size), :], out_ref.at[pl.ds(pl.multiple_of(total, ALIGN), size), :], blank_sem)

    @pl.when(rest > 0)
    def _():
        blank_copy().start()

    gate_copy.wait()

    def stores(k):
        first = pl.multiple_of(place[0, k], ALIGN)
        size = pl.multiple_of(place[1, k], ALIGN)
        used, rows = pl.ds(0, size), pl.ds(first, size)
        return [
            pltpu.make_async_copy(tok.at[k, used, :], out_ref.at[rows, pl.ds(0, 2 * d_model)], out_sem.at[k, 0]),
            pltpu.make_async_copy(gated.at[k, used, :], out_ref.at[rows, pl.ds(2 * d_model, d_model)], out_sem.at[k, 1]),
        ]

    for k in range(pieces):
        loads[k].wait()

        @pl.when(place[1, k] > 0)
        def _():
            def gate_rows(r, carry):
                rows = pl.ds(pl.multiple_of(r * LANES, LANES), LANES)
                for c in range(d_model // LANES):
                    dy = tok[k, rows, pl.ds(d_model + c * LANES, LANES)].astype(F32)
                    gated[k, rows, pl.ds(c * LANES, LANES)] = (gates[k, rows, :] * dy).astype(BF16)
                return carry

            lax.fori_loop(0, (place[1, k] + LANES - 1) // LANES, gate_rows, 0)
            for store in stores(k):
                store.start()

    for k in range(pieces):
        @pl.when(place[1, k] > 0)
        def _():
            for store in stores(k):
                store.wait()

    @pl.when(rest > 0)
    def _():
        blank_copy().wait()


def pack(counts, tokens, gates, capacity, d_model):
    pieces = len(tokens)
    smem = pl.BlockSpec(memory_space=pltpu.SMEM)
    return pl.pallas_call(
        functools.partial(pack_kernel, pieces, d_model),
        out_shape=[jax.ShapeDtypeStruct((pieces * capacity, 3 * d_model), BF16), jax.ShapeDtypeStruct((3, pieces), I32)],
        in_specs=[smem] + [ANY] * (pieces + 1),
        out_specs=[ANY, smem],
        scratch_shapes=[
            pltpu.VMEM((pieces, capacity, 2 * d_model), BF16),
            pltpu.VMEM((pieces, capacity, LANES), F32),
            pltpu.VMEM((pieces, capacity, d_model), BF16),
            pltpu.VMEM((TILE, 3 * d_model), BF16),
            pltpu.SemaphoreType.DMA((pieces,)),
            pltpu.SemaphoreType.DMA,
            pltpu.SemaphoreType.DMA((pieces, 2)),
            pltpu.SemaphoreType.DMA,
        ],
        compiler_params=params(),
        cost_estimate=pl.CostEstimate(flops=10**9, bytes_accessed=40 * 2**20, transcendentals=0),
        name='pack',
    )(counts, *tokens, gates)


def unpack_kernel(pieces, place, packed_ref, *refs):
    out_refs = refs[:pieces]
    rows_ref, in_sem, out_sem = refs[pieces:]
    load = pltpu.make_async_copy(packed_ref, rows_ref, in_sem)
    load.start()
    load.wait()

    def store(k):
        first = pl.multiple_of(place[0, k], ALIGN)
        size = pl.multiple_of(place[1, k], ALIGN)
        return pltpu.make_async_copy(rows_ref.at[pl.ds(first, size), :], out_refs[k].at[pl.ds(0, size), :], out_sem.at[k])

    for k in range(pieces):
        @pl.when(place[1, k] > 0)
        def _():
            store(k).start()
    for k in range(pieces):
        @pl.when(place[1, k] > 0)
        def _():
            store(k).wait()


def unpack(place, packed, pieces, capacity):
    d_model = packed.shape[1]
    return pl.pallas_call(
        functools.partial(unpack_kernel, pieces),
        out_shape=[jax.ShapeDtypeStruct((capacity, d_model), packed.dtype)] * pieces,
        in_specs=[pl.BlockSpec(memory_space=pltpu.SMEM), ANY],
        out_specs=[ANY] * pieces,
        scratch_shapes=[pltpu.VMEM(packed.shape, packed.dtype), pltpu.SemaphoreType.DMA, pltpu.SemaphoreType.DMA((pieces,))],
        compiler_params=params(),
        cost_estimate=pl.CostEstimate(flops=10**9, bytes_accessed=16 * 2**20, transcendentals=0),
        name='unpack',
    )(place, packed)


def expert_kernel(shards, d_model, width, first, last, carry, place, info, *refs):
    refs = list(refs)
    tok_ref = refs.pop(0)
    w_refs = [refs.pop(0) for _ in range(shards)]
    dx_in, dg_in, flip = (None, None, None) if first else (refs.pop(0), refs.pop(0), refs.pop(0))
    old_refs = [refs.pop(0) for _ in range(shards)] if carry else []
    dx_out, dg_out = refs.pop(0), refs.pop(0)
    if first:
        flip = refs.pop(0)
    grad_refs = [refs.pop(0) for _ in range(shards)]
    w_mem, grads, dx_sum, w_sem, old_sem, new_sem = refs
    d_shard = d_model // shards
    step = pl.program_id(0)
    tiles, my_shard = place[2, 0], info[0]
    chunks = width // CHUNK

    def shard_rows(k):
        return pl.ds(pl.multiple_of((my_shard ^ k) * d_shard, ALIGN), d_shard)

    def cols_of(c):
        return pl.ds(c * CHUNK if isinstance(c, int) else pl.multiple_of(c * CHUNK, CHUNK), CHUNK)

    def loads(c):
        found = [pltpu.make_async_copy(w_refs[k].at[:, :, cols_of(c)], w_mem.at[:, shard_rows(k), cols_of(c)], w_sem.at[k, c]) for k in range(shards)]
        return found + [pltpu.make_async_copy(r.at[:, :, cols_of(c)], grads.at[:, shard_rows(k), cols_of(c)], old_sem.at[k, c]) for k, r in enumerate(old_refs)]

    def stores(c):
        return [pltpu.make_async_copy(grads.at[:, shard_rows(k), cols_of(c)], r.at[:, :, cols_of(c)], new_sem.at[k, c]) for k, r in enumerate(grad_refs)]

    @pl.when(step == 0)
    def _():
        for c in range(chunks):
            for copy in loads(c):
                copy.start()
        if not carry:
            grads[...] = jnp.zeros_like(grads)

    @pl.when(step < tiles)
    def _():
        if first:
            flip[0, 0] = tok_ref[:, pl.ds(0, d_model)].T
            flip[0, 1] = tok_ref[:, pl.ds(2 * d_model, d_model)].T
        dx_sum[...] = jnp.zeros_like(dx_sum) if first else dx_in[...]

        def chunk(c, dg):
            @pl.when(step == 0)
            def _():
                for copy in loads(c):
                    copy.wait()

            cols = cols_of(c)
            x, dy, g = (tok_ref[:, pl.ds(j * d_model, d_model)] for j in range(3))
            w_a, w_b, w_c = w_mem[0, :, cols], w_mem[1, :, cols], w_mem[2, :, cols]
            h_one = matmul(x, w_a)
            h_three = matmul(x, w_c)
            y_part = matmul(dy, w_b)
            d_act = matmul(g, w_b)
            sigma = jax.nn.sigmoid(h_one)
            silu = h_one * sigma
            act = (silu * h_three).astype(BF16)
            prod = act.astype(F32) * y_part
            dh_three = (d_act * silu).astype(BF16)
            dh_one = (d_act * h_three * sigma * (1.0 + h_one * (1.0 - sigma))).astype(BF16)
            grads[0, :, cols] += matmul(flip[0, 0], dh_one)
            grads[1, :, cols] += matmul(flip[0, 1], act)
            grads[2, :, cols] += matmul(flip[0, 0], dh_three)
            dx_sum[...] += matmul_nt(dh_one, w_a) + matmul_nt(dh_three, w_c)
            for j in range(CHUNK // LANES):
                dg = dg + prod[:, j * LANES:(j + 1) * LANES]

            @pl.when(step == tiles - 1)
            def _():
                for copy in stores(c):
                    copy.start()

            return dg

        dg = lax.fori_loop(0, chunks, chunk, jnp.zeros((TILE, LANES), F32) if first else dg_in[...])
        dx_out[...] = dx_sum[...].astype(dx_out.dtype)
        if last:
            dg_out[0] = jnp.broadcast_to(jnp.sum(dg.T, axis=0, keepdims=True), (8, TILE))
        else:
            dg_out[...] = dg

    @pl.when((step == 0) & (tiles == 0))
    def _():
        for c in range(chunks):
            for copy in loads(c):
                copy.wait()
        for c in range(chunks):
            for copy in stores(c):
                copy.start()

    @pl.when(step == pl.num_programs(0) - 1)
    def _():
        for c in range(chunks):
            for copy in stores(c):
                copy.wait()


def expert_block(place, info, tok, w_pieces, partial, old, last):
    rows, d_model = tok.shape[0], tok.shape[1] // 3
    shards = len(w_pieces)
    d_shard, width = w_pieces[0].shape[1:]
    first, carry = partial is None, old is not None
    at = lambda i, place: jnp.minimum(i, jnp.maximum(place[2, 0] - 1, 0))
    row_block = lambda i, place, info: (at(i, place), 0)
    dx_spec, dg_spec = pl.BlockSpec((TILE, d_model), row_block), pl.BlockSpec((TILE, LANES), row_block)
    flip_spec = pl.BlockSpec((1, 2, d_model, TILE), lambda i, place, info: (at(i, place), 0, 0, 0))
    flip_shape = jax.ShapeDtypeStruct((rows // TILE, 2, d_model, TILE), BF16)
    ins = [tok] + list(w_pieces) + ([] if first else list(partial)) + (list(old) if carry else [])
    in_specs = [pl.BlockSpec((TILE, 3 * d_model), row_block)] + [ANY] * shards + ([] if first else [dx_spec, dg_spec, flip_spec]) + ([ANY] * shards if carry else [])
    out_shape = [jax.ShapeDtypeStruct((rows, d_model), BF16 if last else F32)]
    out_specs = [dx_spec]
    if last:
        out_shape.append(jax.ShapeDtypeStruct((rows // TILE, 8, TILE), F32))
        out_specs.append(pl.BlockSpec((1, 8, TILE), lambda i, place, info: (at(i, place), 0, 0)))
    else:
        out_shape.append(jax.ShapeDtypeStruct((rows, LANES), F32))
        out_specs.append(dg_spec)
    if first:
        out_shape.append(flip_shape)
        out_specs.append(flip_spec)
    head = len(out_shape)
    aliases = {} if first or last else {2 + 1 + shards: 0, 2 + 1 + shards + 1: 1}
    outs = pl.pallas_call(
        functools.partial(expert_kernel, shards, d_model, width, first, last, carry),
        out_shape=out_shape + [jax.ShapeDtypeStruct((3, d_shard, width), F32)] * shards,
        grid_spec=pltpu.PrefetchScalarGridSpec(
            num_scalar_prefetch=2,
            grid=(rows // TILE,),
            in_specs=in_specs,
            out_specs=out_specs + [ANY] * shards,
            scratch_shapes=[
                pltpu.VMEM((3, d_model, width), BF16),
                pltpu.VMEM((3, d_model, width), F32),
                pltpu.VMEM((TILE, d_model), F32),
                pltpu.SemaphoreType.DMA((shards, width // CHUNK)),
                pltpu.SemaphoreType.DMA((shards, width // CHUNK)),
                pltpu.SemaphoreType.DMA((shards, width // CHUNK)),
            ],
        ),
        input_output_aliases=aliases,
        compiler_params=params(),
        cost_estimate=pl.CostEstimate(flops=18 * (rows * 6 // 10) * d_model * width, bytes_accessed=40 * 2**20, transcendentals=rows * width),
        name='expert',
    )(place, info, *ins)
    flip = outs[2] if first else partial[2]
    return (outs[0], outs[1], flip), outs[head:]


def assemble_kernel(shards, first_col, width, fresh, info, *refs):
    piece_refs = refs[:shards]
    out_refs = refs[shards + (0 if fresh else 3):][:3]
    mem, in_sem, out_sem = refs[-3:]
    my_shard = info[0]
    loads = [pltpu.make_async_copy(piece_refs[k], mem.at[k], in_sem.at[k]) for k in range(shards)]
    stores = [[pltpu.make_async_copy(mem.at[k, j], out_refs[j].at[my_shard ^ k, :, pl.ds(first_col, width)], out_sem.at[k, j]) for j in range(3)] for k in range(shards)]
    for load in loads:
        load.start()
    for k in range(shards):
        loads[k].wait()
        for store in stores[k]:
            store.start()
    for k in range(shards):
        for store in stores[k]:
            store.wait()


def assemble(info, pieces, first_col, width, ff_dim, outs):
    shards = len(pieces)
    d_shard = pieces[0].shape[1]
    fresh = outs is None
    return pl.pallas_call(
        functools.partial(assemble_kernel, shards, first_col, width, fresh),
        out_shape=[jax.ShapeDtypeStruct((shards, d_shard, ff_dim), F32)] * 3,
        in_specs=[pl.BlockSpec(memory_space=pltpu.SMEM)] + [ANY] * (shards + (0 if fresh else 3)),
        out_specs=[ANY] * 3,
        scratch_shapes=[pltpu.VMEM((shards, 3, d_shard, width), F32), pltpu.SemaphoreType.DMA((shards,)), pltpu.SemaphoreType.DMA((shards, 3))],
        input_output_aliases={} if fresh else {1 + shards + j: j for j in range(3)},
        compiler_params=params(),
        cost_estimate=pl.CostEstimate(flops=10**9, bytes_accessed=20 * 2**20, transcendentals=0),
        name='assemble',
    )(info, *pieces, *([] if fresh else outs))


def solution(mesh):
    shards, ep_size = mesh.shape['fsdp'], mesh.shape['ep']
    devices = shards * ep_size
    tok_spec = P(None, BOTH, None)
    spec_edf = P('ep', 'fsdp', None)
    spec_efd = P('ep', None, 'fsdp')

    def local_step(x_in, dy_out, expert_idx, gate_prob, w_one, w_two, w_three):
        micro, tok_rows, d_model = x_in.shape
        top_k = expert_idx.shape[2]
        local_experts, d_shard, ff_dim = w_one.shape
        assert local_experts == shards
        capacity = capacity_of(tok_rows, top_k, devices)
        slots = devices * capacity
        blk = ff_dim // BLOCKS
        my_shard = lax.axis_index('fsdp').astype(I32)
        me = my_shard * ep_size + lax.axis_index('ep').astype(I32)
        shard_info, device_info = my_shard[None], me[None]

        w_all = [w_one, jnp.swapaxes(w_two, 1, 2), w_three]

        def send_weights(b):
            pieces = []
            for k in range(shards):
                cut = [lax.dynamic_slice(w, (my_shard ^ k, 0, b * blk), (1, d_shard, blk))[0] for w in w_all]
                pieces.append(swap(jnp.stack(cut), 'fsdp', k, shards))
            return pieces

        w_blocks = [send_weights(b) for b in range(BLOCKS)]

        ids = jnp.transpose(expert_idx, (0, 2, 1))
        gate_rows = jnp.transpose(gate_prob, (0, 2, 1))
        sent_tok, sent_gate, slots_of = [], [], []
        for m in range(micro):
            rows, gates, slot = dispatch(device_info, ids[m], gate_rows[m], x_in, dy_out, m, devices, local_experts, ep_size, capacity)
            slots_of.append(slot)
            sent_gate.append(jnp.stack([swap(gates[k], BOTH, k, devices) for k in range(devices)]))
            sent_tok.append([swap(rows[k], BOTH, k, devices) for k in range(devices)])

        zero_row = jnp.zeros((1, d_model), BF16)
        dx_parts, dg_parts = [], []
        grads = [None] * BLOCKS
        outs = None
        for m in range(micro):
            gates = sent_gate[m]
            counts = gates[:, capacity].astype(I32)
            gate_wide = jnp.broadcast_to(gates[:, :capacity, None], (devices, capacity, LANES))
            tok, place = pack(counts, sent_tok[m], gate_wide, capacity, d_model)
            partial = None
            for b in range(BLOCKS):
                partial, grads[b] = expert_block(place, shard_info, tok, w_blocks[b], partial, grads[b], b == BLOCKS - 1)
            back = unpack(place, partial[0], devices, capacity)
            note = jnp.concatenate([partial[1][:, 0, :].reshape(-1), place[0].astype(F32), jnp.zeros((LANES - devices,), F32)])
            back = [swap(v, BOTH, k, devices) for k, v in enumerate(back)]
            notes = [swap(note, BOTH, k, devices) for k in range(devices)]
            back = jnp.concatenate(back + [zero_row])
            notes = jnp.stack(notes)
            slot = slots_of[m]
            total_dx = sum(back[slot[j]].astype(F32) for j in range(top_k))
            dx_parts.append(total_dx.astype(BF16))
            first_row = jnp.stack([notes[k, slots + k] for k in range(devices)]).astype(I32)
            shift = first_row + jnp.arange(devices, dtype=I32) * notes.shape[1]
            piece, position = slot // capacity, slot % capacity
            where_dg = position + jnp.sum(jnp.where(piece[..., None] == jnp.arange(devices), shift, 0), axis=-1)
            dg = jnp.where(piece < devices, notes.reshape(-1)[jnp.where(piece < devices, where_dg, 0)], 0.0)
            dg_parts.append(jnp.transpose(dg))
        for b in range(BLOCKS):
            moved = [swap(v, 'fsdp', k, shards) for k, v in enumerate(grads[b])]
            outs = assemble(shard_info, moved, b * blk, blk, ff_dim, outs)
        dw_one, dw_two, dw_three = outs
        return jnp.stack(dx_parts), jnp.stack(dg_parts), dw_one, jnp.swapaxes(dw_two, 1, 2), dw_three

    return jax.shard_map(local_step, mesh=mesh, in_specs=(tok_spec, tok_spec, tok_spec, tok_spec, spec_edf, spec_efd, spec_edf), out_specs=(tok_spec, tok_spec, spec_edf, spec_efd, spec_edf), check_vma=False)
```

time: 2040 us -> 1860 us (0.912)
  local copies, waits for them, and re-layouts: 413 us -> 231 us
  between operations: 34.3 us -> 2.22 us
  waiting for transfers between devices: 686 us -> 715 us
  Pallas kernels: 740 us -> 768 us
    gather x24 -> x8, local copies, waits for them, and re-layouts: 310 us -> 138 us  [the longest x4 82.7 us: local_step(): notes.reshape(-1)[jnp.where(piece < devices, where_dg, 0)]]
    pallas_call x0 -> x2, Pallas kernels: none -> 72.8 us  [dispatch(): pl.pallas_call(functools.partial(dispatch_kernel, pieces, local_experts,...]
    pallas_call x8, Pallas kernels: 671 us -> 623 us  [expert_block(): pl.pallas_call(functools.partial(expert_kernel, shards, d_model, width, f...]
    scatter x2 -> x0, local copies, waits for them, and re-layouts: 31.6 us -> none  [local_step(): jnp.full((slots + 1,), n_choice, I32).at[choice_slot[m]]]
    ppermute x74 -> x80, waiting for transfers between devices: 686 us -> 715 us  [swap(): return lax.ppermute(value, axes, [(s, s ^ shift) for s in range(devices)])]
    ppermute x74 -> x80, starting transfers between devices: 111 us -> 97.4 us  [swap(): return lax.ppermute(value, axes, [(s, s ^ shift) for s in range(devices)])]
    unnamed x147 -> x206, local copies, waits for them, and re-layouts: 32.7 us -> 41.3 us
  transfers between devices with their start and end apart: 74 -> 80, of which waited for: 23 -> 23; matrix products, arithmetic and copies ran while one was open for 20% -> 14% of each run, Pallas kernels for 29% -> 39%
where the time goes in v1:
time: 1860 us; the launch traced here: 1850 us
  Pallas kernels  768 us (41%)
  waiting for transfers between devices  715 us (38%)
  local copies, waits for them, and re-layouts  231 us (12%)
  starting transfers between devices  97.4 us (5%)
  other arithmetic  35.1 us (2%)
    ppermute x80, waiting for transfers between devices, swap(): return lax.ppermute(value, axes, [(s, s ^ shift) for s in range(devices)])  715 us
    pallas_call x8, Pallas kernels, expert_block(): pl.pallas_call(functools.partial(expert_kernel, shards, d_model, width, f...  623 us
    ppermute x80, starting transfers between devices, swap(): return lax.ppermute(value, axes, [(s, s ^ shift) for s in range(devices)])  97.4 us
    gather x4, local copies, waits for them, and re-layouts, local_step(): notes.reshape(-1)[jnp.where(piece < devices, where_dg, 0)]  82.7 us
    pallas_call x2, Pallas kernels, dispatch(): pl.pallas_call(functools.partial(dispatch_kernel, pieces, local_experts,...  72.8 us
    gather x4, local copies, waits for them, and re-layouts, local_step(): total_dx = sum((back[slot[j]].astype(F32) for j in range(top_k)))  55.8 us
    unnamed x206, local copies, waits for them, and re-layouts  41.3 us
  transfers between devices with their start and end apart: 80, of which 23 were waited for; matrix products, arithmetic and copies ran while one was open for 14% of the time, Pallas kernels for 39%

profile of v1, /device:TPU:0, one launch (start us, length us, event | category | flops | bytes accessed | tf_op | source)
XLA Modules:
  0.0 1848.5 jit_solution(9290914459410343124)
XLA Ops:
  3.3 37.5 %dispatch.2 = (bf16[640,1536]{1,0:T(8,128)(2,1)}, bf16[640,1536]{1,0:T(8,128)(2,1)}, bf16[640,1536]{1,0:T(8,128)(2,1)}, bf16[640,1536]{1,0:T(8,128)(2,1)}, bf16[...) custom-call(s32[1]{0:T(128)} %bitcast.info, ...), custom_call_target="tpu_custom_call" | custom-call | flops 32212254720 | bytes 25165824 | tf_op jit(solution)/shard_map/dispatch/pallas_call | solution.py:123
  45.6 35.2 %dispatch.3 = (bf16[640,1536]{1,0:T(8,128)(2,1)}, bf16[640,1536]{1,0:T(8,128)(2,1)}, bf16[640,1536]{1,0:T(8,128)(2,1)}, bf16[640,1536]{1,0:T(8,128)(2,1)}, bf16[...) custom-call(s32[1]{0:T(128)} %bitcast.info, ...), custom_call_target="tpu_custom_call" | custom-call | flops 32212254720 | bytes 25165824 | tf_op jit(solution)/shard_map/dispatch/pallas_call | solution.py:123
  145.1 85.4 %collective-permute-done.10.refs_4_ = bf16[640,1536]{1,0:T(8,128)(2,1)S(1)} collective-permute-done((bf16[640,1536]{1,0:T(8,128)(2,1)}, bf16[640,1536]{1,0:T(8,128)(2,1)S(1)}, u32[]{:S(2)}, u32[]{:S(2)}) %collective-permute-start.10) | collective-permute-done | bytes 1966112 | tf_op jit(solution)/shard_map/ppermute | solution.py:30
  231.5 40.2 %collective-permute-done.11.refs_5_ = bf16[640,1536]{1,0:T(8,128)(2,1)S(1)} collective-permute-done((bf16[640,1536]{1,0:T(8,128)(2,1)}, bf16[640,1536]{1,0:T(8,128)(2,1)S(1)}, u32[]{:S(2)}, u32[]{:S(2)}) %collective-permute-start.11) | collective-permute-done | bytes 1966112 | tf_op jit(solution)/shard_map/ppermute | solution.py:30
  298.7 24.6 %collective-permute-done.24.refs_3_ = bf16[3,192,1024]{2,1,0:T(8,128)(2,1)} collective-permute-done((bf16[3,192,1024]{2,1,0:T(8,128)(2,1)}, bf16[3,192,1024]{2,1,0:T(8,128)(2,1)}, u32[]{:S(2)}, u32[]{:S(2)}) %collective-permute-start.24) | collective-permute-done | bytes 1179680 | tf_op jit(solution)/shard_map/ppermute | solution.py:30
  326.9 64.0 %expert.8 = (f32[5120,768]{1,0:T(8,128)}, f32[5120,128]{1,0:T(8,128)}, bf16[10,2,768,512]{3,2,1,0:T(8,128)(2,1)}, f32[3,192,1024]{2,1,0:T(8,128)}, f32[3,192,102...) custom-call(s32[3,8]{1,0:T(4,128)} %get-tuple-element.116.place, s32[1]{0:T(128)} %bitcast.5.info, ...), custom_call_target="tpu_custom_call" | custom-call | flops 43486543872 | bytes 41943040 | tf_op jit(solution)/shard_map/expert/pallas_call | solution.py:392
  402.5 63.3 %expert.9 = (f32[5120,768]{1,0:T(8,128)}, f32[5120,128]{1,0:T(8,128)}, f32[3,192,1024]{2,1,0:T(8,128)}, f32[3,192,1024]{2,1,0:T(8,128)}, f32[3,192,1024]{2,1,0:T(8,128)}, /*index=5*/f32[3,192,1024]{2,1,0:T(8,128)}) custom-call(s32[3,8]{1,0:T(4,128)} %get-tuple-element.116.place, s32[1]{0:T(128)} %bitcast.5.info, ...), custom_call_target="tpu_custom_call", output_to_operand_aliasing={{0}: (7, {}), {1}: (8, {})} | custom-call | flops 43486543872 | bytes 41943040 | tf_op jit(solution)/shard_map/expert/pallas_call | solution.py:392
  478.0 63.3 %expert.10 = (f32[5120,768]{1,0:T(8,128)}, f32[5120,128]{1,0:T(8,128)}, f32[3,192,1024]{2,1,0:T(8,128)}, f32[3,192,1024]{2,1,0:T(8,128)}, f32[3,192,1024]{2,1,0:T(8,128)}, /*index=5*/f32[3,192,1024]{2,1,0:T(8,128)}) custom-call(s32[3,8]{1,0:T(4,128)} %get-tuple-element.116.place, s32[1]{0:T(128)} %bitcast.5.info, ...), custom_call_target="tpu_custom_call", output_to_operand_aliasing={{0}: (7, {}), {1}: (8, {})} | custom-call | flops 43486543872 | bytes 41943040 | tf_op jit(solution)/shard_map/expert/pallas_call | solution.py:392
  556.7 63.2 %expert.11 = (bf16[5120,768]{1,0:T(8,128)(2,1)}, f32[10,8,512]{2,1,0:T(8,128)}, f32[3,192,1024]{2,1,0:T(8,128)}, f32[3,192,1024]{2,1,0:T(8,128)}, f32[3,192,1024]{2,1,0:T(8,128)}, /*index=5*/f32[3,192,1024]{2,1,0:T(8,128)}) custom-call(s32[3,8]{1,0:T(4,128)} %get-tuple-element.116.place, s32[1]{0:T(128)} %bitcast.5.info, ...), custom_call_target="tpu_custom_call" | custom-call | flops 43486543872 | bytes 41943040 | tf_op jit(solution)/shard_map/expert/pallas_call | solution.py:392
  622.1 61.2 %collective-permute-done.43.refs_4_ = bf16[640,1536]{1,0:T(8,128)(2,1)} collective-permute-done((bf16[640,1536]{1,0:T(8,128)(2,1)}, bf16[640,1536]{1,0:T(8,128)(2,1)}, u32[]{:S(2)}, u32[]{:S(2)}) %collective-permute-start.43) | collective-permute-done | bytes 1966112 | tf_op jit(solution)/shard_map/ppermute | solution.py:30
  683.4 37.9 %collective-permute-done.44.refs_5_ = bf16[640,1536]{1,0:T(8,128)(2,1)} collective-permute-done((bf16[640,1536]{1,0:T(8,128)(2,1)}, bf16[640,1536]{1,0:T(8,128)(2,1)}, u32[]{:S(2)}, u32[]{:S(2)}) %collective-permute-start.44) | collective-permute-done | bytes 1966112 | tf_op jit(solution)/shard_map/ppermute | solution.py:30
  742.5 93.8 %expert.12 = (f32[5120,768]{1,0:T(8,128)}, f32[5120,128]{1,0:T(8,128)}, bf16[10,2,768,512]{3,2,1,0:T(8,128)(2,1)}, f32[3,192,1024]{2,1,0:T(8,128)}, f32[3,192,10...) custom-call(s32[3,8]{1,0:T(4,128)} %get-tuple-element.144.place, s32[1]{0:T(128)} %bitcast.5.info, ...), custom_call_target="tpu_custom_call" | custom-call | flops 43486543872 | bytes 41943040 | tf_op jit(solution)/shard_map/expert/pallas_call | solution.py:392
  836.3 91.8 %expert.13 = (f32[5120,768]{1,0:T(8,128)}, f32[5120,128]{1,0:T(8,128)}, f32[3,192,1024]{2,1,0:T(8,128)}, f32[3,192,1024]{2,1,0:T(8,128)}, f32[3,192,1024]{2,1,0:T(8,128)}, /*index=5*/f32[3,192,1024]{2,1,0:T(8,128)}) custom-call(s32[3,8]{1,0:T(4,128)} %get-tuple-element.144.place, s32[1]{0:T(128)} %bitcast.5.info, ...), custom_call_target="tpu_custom_call", output_to_operand_aliasing={{0}: (7, {}), {1}: (8, {})} | custom-call | flops 43486543872 | bytes 41943040 | tf_op jit(solution)/shard_map/expert/pallas_call | solution.py:392
  928.1 91.9 %expert.14 = (f32[5120,768]{1,0:T(8,128)}, f32[5120,128]{1,0:T(8,128)}, f32[3,192,1024]{2,1,0:T(8,128)}, f32[3,192,1024]{2,1,0:T(8,128)}, f32[3,192,1024]{2,1,0:T(8,128)}, /*index=5*/f32[3,192,1024]{2,1,0:T(8,128)}) custom-call(s32[3,8]{1,0:T(4,128)} %get-tuple-element.144.place, s32[1]{0:T(128)} %bitcast.5.info, ...), custom_call_target="tpu_custom_call", output_to_operand_aliasing={{0}: (7, {}), {1}: (8, {})} | custom-call | flops 43486543872 | bytes 41943040 | tf_op jit(solution)/shard_map/expert/pallas_call | solution.py:392
  1020.0 91.8 %expert.15 = (bf16[5120,768]{1,0:T(8,128)(2,1)}, f32[10,8,512]{2,1,0:T(8,128)}, f32[3,192,1024]{2,1,0:T(8,128)}, f32[3,192,1024]{2,1,0:T(8,128)}, f32[3,192,1024]{2,1,0:T(8,128)}, /*index=5*/f32[3,192,1024]{2,1,0:T(8,128)}) custom-call(s32[3,8]{1,0:T(4,128)} %get-tuple-element.144.place, s32[1]{0:T(128)} %bitcast.5.info, ...), custom_call_target="tpu_custom_call" | custom-call | flops 43486543872 | bytes 41943040 | tf_op jit(solution)/shard_map/expert/pallas_call | solution.py:392
  1130.0 42.0 %collective-permute-done.62 = f32[5248]{0:T(1024)S(1)} collective-permute-done((f32[5248]{0:T(1024)S(1)}, f32[5248]{0:T(1024)S(1)}, u32[]{:S(2)}, u32[]{:S(2)}) %collective-permute-start.62) | collective-permute-done | bytes 21024 | tf_op jit(solution)/shard_map/ppermute | solution.py:30
  1184.6 55.0 %collective-permute-done.29 = bf16[640,768]{1,0:T(8,128)(2,1)S(1)} collective-permute-done((bf16[640,768]{1,0:T(8,128)(2,1)}, bf16[640,768]{1,0:T(8,128)(2,1)S(1)}, u32[]{:S(2)}, u32[]{:S(2)}) %collective-permute-start.29) | collective-permute-done | bytes 983072 | tf_op jit(solution)/shard_map/ppermute | solution.py:30
  1296.9 69.8 %collective-permute-done.48 = bf16[640,768]{1,0:T(8,128)(2,1)} collective-permute-done((bf16[640,768]{1,0:T(8,128)(2,1)}, bf16[640,768]{1,0:T(8,128)(2,1)}, u32[]{:S(2)}, u32[]{:S(2)}) %collective-permute-start.48) | collective-permute-done | bytes 983072 | tf_op jit(solution)/shard_map/ppermute | solution.py:30
  1390.6 40.5 %gather_fusion.4 = f32[4096]{0:T(1024)} fusion(f32[41984]{0:T(1024)S(1)} %reshape.184, s32[4096]{0:T(1024)} %broadcast_clamp_fusion.1), kind=kCustom, calls=%fused_computation.4 | custom fusion | bytes 49152 | tf_op jit(solution)/shard_map/gather | solution.py:517
  1439.6 40.7 %gather_fusion.5 = f32[4096]{0:T(1024)} fusion(f32[41984]{0:T(1024)S(1)} %reshape.185, s32[4096]{0:T(1024)} %broadcast_clamp_fusion), kind=kCustom, calls=%fused_computation.5 | custom fusion | bytes 49152 | tf_op jit(solution)/shard_map/gather | solution.py:517
  1507.0 32.3 %collective-permute-done.75.refs_2_ = f32[3,192,1024]{2,1,0:T(8,128)} collective-permute-done((f32[3,192,1024]{2,1,0:T(8,128)}, f32[3,192,1024]{2,1,0:T(8,128)}, u32[]{:S(2)}, u32[]{:S(2)}) %collective-permute-start.75) | collective-permute-done | bytes 2359328 | tf_op jit(solution)/shard_map/ppermute | solution.py:30
  1570.5 119.5 %collective-permute-done.78.refs_2_ = f32[3,192,1024]{2,1,0:T(8,128)} collective-permute-done((f32[3,192,1024]{2,1,0:T(8,128)}, f32[3,192,1024]{2,1,0:T(8,128)}, u32[]{:S(2)}, u32[]{:S(2)}) %collective-permute-start.78) | collective-permute-done | bytes 2359328 | tf_op jit(solution)/shard_map/ppermute | solution.py:30
  1749.6 41.4 %collective-permute-done.72.refs_2_ = f32[3,192,1024]{2,1,0:T(8,128)} collective-permute-done((f32[3,192,1024]{2,1,0:T(8,128)}, f32[3,192,1024]{2,1,0:T(8,128)}, u32[]{:S(2)}, u32[]{:S(2)}) %collective-permute-start.72) | collective-permute-done | bytes 2359328 | tf_op jit(solution)/shard_map/ppermute | solution.py:30
  1798.9 41.5 %collective-permute-done.69.refs_2_ = f32[3,192,1024]{2,1,0:T(8,128)} collective-permute-done((f32[3,192,1024]{2,1,0:T(8,128)}, f32[3,192,1024]{2,1,0:T(8,128)}, u32[]{:S(2)}, u32[]{:S(2)}) %collective-permute-start.69) | collective-permute-done | bytes 2359328 | tf_op jit(solution)/shard_map/ppermute | solution.py:30
  (481 shorter events, 418.4 us)
Async XLA Ops:
  101.9 169.8 %collective-permute-start.11 = (bf16[640,1536]{1,0:T(8,128)(2,1)}, bf16[640,1536]{1,0:T(8,128)(2,1)S(1)}, u32[]{:S(2)}, u32[]{:S(2)}) collective-permute-start(bf16[640,1536]{1,0:T(8,128)(2,1)} %get-tuple-element.113), channel_id=1, source_target_pairs={{0,5},{1,4},{2,7},{3,6},{4,1},{5,0},{6,3},{7,2}} | collective-permute-start | bytes 5898248 | tf_op jit(solution)/shard_map/ppermute | solution.py:30
  116.0 165.7 %collective-permute-start.12 = (bf16[640,1536]{1,0:T(8,128)(2,1)}, bf16[640,1536]{1,0:T(8,128)(2,1)}, u32[]{:S(2)}, u32[]{:S(2)}) collective-permute-start(bf16[640,1536]{1,0:T(8,128)(2,1)} %get-tuple-element.114), channel_id=1, source_target_pairs={{0,6},{1,7},{2,4},{3,5},{4,2},{5,3},{6,0},{7,1}} | collective-permute-start | bytes 5898248 | tf_op jit(solution)/shard_map/ppermute | solution.py:30
  116.8 166.6 %collective-permute-start.13 = (bf16[640,1536]{1,0:T(8,128)(2,1)}, bf16[640,1536]{1,0:T(8,128)(2,1)}, u32[]{:S(2)}, u32[]{:S(2)}) collective-permute-start(bf16[640,1536]{1,0:T(8,128)(2,1)} %get-tuple-element.115), channel_id=1, source_target_pairs={{0,7},{1,6},{2,5},{3,4},{4,3},{5,2},{6,1},{7,0}} | collective-permute-start | bytes 5898248 | tf_op jit(solution)/shard_map/ppermute | solution.py:30
  144.0 179.4 %collective-permute-start.24 = (bf16[3,192,1024]{2,1,0:T(8,128)(2,1)}, bf16[3,192,1024]{2,1,0:T(8,128)(2,1)}, u32[]{:S(2)}, u32[]{:S(2)}) collective-permute-start(bf16[3,192,1024]{2,1,0:T(8,128)(2,1)} %pad_maximum_fusion.15), channel_id=1, source_target_pairs={{0,4},{2,6},{4,0},{6,2},{1,5},{3,7},{5,1},{7,3}} | collective-permute-start | bytes 3538952 | tf_op jit(solution)/shard_map/ppermute | solution.py:30
  281.7 259.6 %collective-permute-start.14 = (bf16[3,192,1024]{2,1,0:T(8,128)(2,1)}, bf16[3,192,1024]{2,1,0:T(8,128)(2,1)}, u32[]{:S(2)}, u32[]{:S(2)}) collective-permute-start(bf16[3,192,1024]{2,1,0:T(8,128)(2,1)} %pad_maximum_fusion.2), channel_id=1, source_target_pairs={{0,2},{2,0},{4,6},{6,4},{1,3},{3,1},{5,7},{7,5}} | collective-permute-start | bytes 3538952 | tf_op jit(solution)/shard_map/ppermute | solution.py:30
  283.4 268.9 %collective-permute-start.15 = (bf16[3,192,1024]{2,1,0:T(8,128)(2,1)}, bf16[3,192,1024]{2,1,0:T(8,128)(2,1)}, u32[]{:S(2)}, u32[]{:S(2)}) collective-permute-start(bf16[3,192,1024]{2,1,0:T(8,128)(2,1)} %pad_maximum_fusion.3), channel_id=1, source_target_pairs={{0,4},{2,6},{4,0},{6,2},{1,5},{3,7},{5,1},{7,3}} | collective-permute-start | bytes 3538952 | tf_op jit(solution)/shard_map/ppermute | solution.py:30
  552.3 131.1 %collective-permute-start.43 = (bf16[640,1536]{1,0:T(8,128)(2,1)}, bf16[640,1536]{1,0:T(8,128)(2,1)}, u32[]{:S(2)}, u32[]{:S(2)}) collective-permute-start(bf16[640,1536]{1,0:T(8,128)(2,1)} %get-tuple-element.140), channel_id=1, source_target_pairs={{0,4},{1,5},{2,6},{3,7},{4,0},{5,1},{6,2},{7,3}} | collective-permute-start | bytes 5898248 | tf_op jit(solution)/shard_map/ppermute | solution.py:30
  552.3 169.0 %collective-permute-start.44 = (bf16[640,1536]{1,0:T(8,128)(2,1)}, bf16[640,1536]{1,0:T(8,128)(2,1)}, u32[]{:S(2)}, u32[]{:S(2)}) collective-permute-start(bf16[640,1536]{1,0:T(8,128)(2,1)} %get-tuple-element.141), channel_id=1, source_target_pairs={{0,5},{1,4},{2,7},{3,6},{4,1},{5,0},{6,3},{7,2}} | collective-permute-start | bytes 5898248 | tf_op jit(solution)/shard_map/ppermute | solution.py:30
  552.4 170.8 %collective-permute-start.45 = (bf16[640,1536]{1,0:T(8,128)(2,1)}, bf16[640,1536]{1,0:T(8,128)(2,1)}, u32[]{:S(2)}, u32[]{:S(2)}) collective-permute-start(bf16[640,1536]{1,0:T(8,128)(2,1)} %get-tuple-element.142), channel_id=1, source_target_pairs={{0,6},{1,7},{2,4},{3,5},{4,2},{5,3},{6,0},{7,1}} | collective-permute-start | bytes 5898248 | tf_op jit(solution)/shard_map/ppermute | solution.py:30
  554.1 170.9 %collective-permute-start.46 = (bf16[640,1536]{1,0:T(8,128)(2,1)}, bf16[640,1536]{1,0:T(8,128)(2,1)}, u32[]{:S(2)}, u32[]{:S(2)}) collective-permute-start(bf16[640,1536]{1,0:T(8,128)(2,1)} %get-tuple-element.143), channel_id=1, source_target_pairs={{0,7},{1,6},{2,5},{3,4},{4,3},{5,2},{6,1},{7,0}} | collective-permute-start | bytes 5898248 | tf_op jit(solution)/shard_map/ppermute | solution.py:30
  622.1 491.3 %collective-permute-start.60 = (f32[5248]{0:T(1024)}, f32[5248]{0:T(1024)}, u32[]{:S(2)}, u32[]{:S(2)}) collective-permute-start(f32[5248]{0:T(1024)} %concatenate.14), channel_id=1, source_target_pairs={{0,7},{1,6},{2,5},{3,4},{4,3},{5,2},{6,1},{7,0}} | collective-permute-start | bytes 62984 | tf_op jit(solution)/shard_map/ppermute | solution.py:30
  683.4 430.1 %collective-permute-start.59 = (f32[5248]{0:T(1024)}, f32[5248]{0:T(1024)}, u32[]{:S(2)}, u32[]{:S(2)}) collective-permute-start(f32[5248]{0:T(1024)} %concatenate.14), channel_id=1, source_target_pairs={{0,6},{1,7},{2,4},{3,5},{4,2},{5,3},{6,0},{7,1}} | collective-permute-start | bytes 62984 | tf_op jit(solution)/shard_map/ppermute | solution.py:30
  721.3 392.2 %collective-permute-start.58 = (f32[5248]{0:T(1024)}, f32[5248]{0:T(1024)}, u32[]{:S(2)}, u32[]{:S(2)}) collective-permute-start(f32[5248]{0:T(1024)} %concatenate.14), channel_id=1, source_target_pairs={{0,5},{1,4},{2,7},{3,6},{4,1},{5,0},{6,3},{7,2}} | collective-permute-start | bytes 62984 | tf_op jit(solution)/shard_map/ppermute | solution.py:30
  723.2 390.3 %collective-permute-start.57 = (f32[5248]{0:T(1024)}, f32[5248]{0:T(1024)}, u32[]{:S(2)}, u32[]{:S(2)}) collective-permute-start(f32[5248]{0:T(1024)} %concatenate.14), channel_id=1, source_target_pairs={{0,4},{1,5},{2,6},{3,7},{4,0},{5,1},{6,2},{7,3}} | collective-permute-start | bytes 62984 | tf_op jit(solution)/shard_map/ppermute | solution.py:30
  724.9 391.6 %collective-permute-start.56 = (f32[5248]{0:T(1024)}, f32[5248]{0:T(1024)}, u32[]{:S(2)}, u32[]{:S(2)}) collective-permute-start(f32[5248]{0:T(1024)} %concatenate.14), channel_id=1, source_target_pairs={{0,3},{1,2},{2,1},{3,0},{4,7},{5,6},{6,5},{7,4}} | collective-permute-start | bytes 62984 | tf_op jit(solution)/shard_map/ppermute | solution.py:30
  1240.6 240.9 %collective-permute-start.71 = (f32[3,192,1024]{2,1,0:T(8,128)}, f32[3,192,1024]{2,1,0:T(8,128)S(1)}, u32[]{:S(2)}, u32[]{:S(2)}) collective-permute-start(f32[3,192,1024]{2,1,0:T(8,128)} %get-tuple-element.186), channel_id=1, source_target_pairs={{0,2},{2,0},{4,6},{6,4},{1,3},{3,1},{5,7},{7,5}} | collective-permute-start | bytes 7077896 | tf_op jit(solution)/shard_map/ppermute | solution.py:30
  1256.7 225.5 %collective-permute-start.74 = (f32[3,192,1024]{2,1,0:T(8,128)}, f32[3,192,1024]{2,1,0:T(8,128)}, u32[]{:S(2)}, u32[]{:S(2)}) collective-permute-start(f32[3,192,1024]{2,1,0:T(8,128)} %get-tuple-element.190), channel_id=1, source_target_pairs={{0,2},{2,0},{4,6},{6,4},{1,3},{3,1},{5,7},{7,5}} | collective-permute-start | bytes 7077896 | tf_op jit(solution)/shard_map/ppermute | solution.py:30
  1481.5 208.4 %collective-permute-start.78 = (f32[3,192,1024]{2,1,0:T(8,128)}, f32[3,192,1024]{2,1,0:T(8,128)}, u32[]{:S(2)}, u32[]{:S(2)}) collective-permute-start(f32[3,192,1024]{2,1,0:T(8,128)} %get-tuple-element.195), channel_id=1, source_target_pairs={{0,4},{2,6},{4,0},{6,2},{1,5},{3,7},{5,1},{7,3}} | collective-permute-start | bytes 7077896 | tf_op jit(solution)/shard_map/ppermute | solution.py:30
  1482.2 208.4 %collective-permute-start.79 = (f32[3,192,1024]{2,1,0:T(8,128)}, f32[3,192,1024]{2,1,0:T(8,128)}, u32[]{:S(2)}, u32[]{:S(2)}) collective-permute-start(f32[3,192,1024]{2,1,0:T(8,128)} %get-tuple-element.196), channel_id=1, source_target_pairs={{0,6},{2,4},{4,2},{6,0},{1,7},{3,5},{5,3},{7,1}} | collective-permute-start | bytes 7077896 | tf_op jit(solution)/shard_map/ppermute | solution.py:30
  1539.3 251.7 %collective-permute-start.72 = (f32[3,192,1024]{2,1,0:T(8,128)}, f32[3,192,1024]{2,1,0:T(8,128)}, u32[]{:S(2)}, u32[]{:S(2)}) collective-permute-start(f32[3,192,1024]{2,1,0:T(8,128)} %get-tuple-element.187), channel_id=1, source_target_pairs={{0,4},{2,6},{4,0},{6,2},{1,5},{3,7},{5,1},{7,3}} | collective-permute-start | bytes 7077896 | tf_op jit(solution)/shard_map/ppermute | solution.py:30
  1539.5 251.5 %collective-permute-start.73 = (f32[3,192,1024]{2,1,0:T(8,128)}, f32[3,192,1024]{2,1,0:T(8,128)}, u32[]{:S(2)}, u32[]{:S(2)}) collective-permute-start(f32[3,192,1024]{2,1,0:T(8,128)} %get-tuple-element.188), channel_id=1, source_target_pairs={{0,6},{2,4},{4,2},{6,0},{1,7},{3,5},{5,3},{7,1}} | collective-permute-start | bytes 7077896 | tf_op jit(solution)/shard_map/ppermute | solution.py:30
  1570.1 228.8 %collective-permute-start.68 = (f32[3,192,1024]{2,1,0:T(8,128)}, f32[3,192,1024]{2,1,0:T(8,128)}, u32[]{:S(2)}, u32[]{:S(2)}) collective-permute-start(f32[3,192,1024]{2,1,0:T(8,128)} %get-tuple-element.182), channel_id=1, source_target_pairs={{0,2},{2,0},{4,6},{6,4},{1,3},{3,1},{5,7},{7,5}} | collective-permute-start | bytes 7077896 | tf_op jit(solution)/shard_map/ppermute | solution.py:30
  1689.9 150.5 %collective-permute-start.69 = (f32[3,192,1024]{2,1,0:T(8,128)}, f32[3,192,1024]{2,1,0:T(8,128)}, u32[]{:S(2)}, u32[]{:S(2)}) collective-permute-start(f32[3,192,1024]{2,1,0:T(8,128)} %get-tuple-element.183), channel_id=1, source_target_pairs={{0,4},{2,6},{4,0},{6,2},{1,5},{3,7},{5,1},{7,3}} | collective-permute-start | bytes 7077896 | tf_op jit(solution)/shard_map/ppermute | solution.py:30
  1690.7 149.8 %collective-permute-start.70 = (f32[3,192,1024]{2,1,0:T(8,128)}, f32[3,192,1024]{2,1,0:T(8,128)}, u32[]{:S(2)}, u32[]{:S(2)}) collective-permute-start(f32[3,192,1024]{2,1,0:T(8,128)} %get-tuple-element.184), channel_id=1, source_target_pairs={{0,6},{2,4},{4,2},{6,0},{1,7},{3,5},{5,3},{7,1}} | collective-permute-start | bytes 7077896 | tf_op jit(solution)/shard_map/ppermute | solution.py:30
  (151 other events, 5483.8 us)
